TPU v7x, 32 devices: a whole 2x2x4 slice. The times are simulated.
32 devices in a mesh: space: 16 (over z, y, core), tm: 2 (over x).
Axes of the slice: x: 2, y: 2, z: 4, core: 2. Of those that a mesh axis runs over, the one named last changes fastest.
Arguments:
- row_orbitals: bfloat16 [8192, 2048], P('space', 'tm'), may hold values from -0.890625 to 0.890625
- column_orbitals: bfloat16 [256, 2048], P('space', 'tm'), may hold values from -0.890625 to 0.890625
- occupation: int32 [2048], replicated, may hold values from 0 to 2
- order: int32 [2048], replicated, may hold values from 0 to 2047, each once
- levels: float32 [2048], replicated, may hold values from 0.1 to 1
- times: float32 [2], replicated, may hold values from 0.05 to 1.5
- quad_weights: float32 [2], replicated, may hold values from 0.5 to 1.5
- freqs: float32 [8], replicated, may hold values from 0.1 to 4
Outputs:
- spectrum: float32 [8, 8192, 256], P(None, ('space', 'tm'))
Inputs may be any that keep to these rules, and one draw needn't show every extreme that they name: `order`: each index of 0 to 2047 once.
All inputs are finite; a program needn't handle non-finite values.
Results may differ from a plain program's by a relative error of at most 0.0026.
Values may be sent and summed in bfloat16 or wider, within the bound.
No kernel may reach another device: no remote copies, remote signals or barrier semaphores. Data moves between devices by JAX's collectives and lax.ppermute only.
A program may use at most 64 MiB of HBM per device.

v0:
```python
import jax
import jax.numpy as jnp
from jax import lax
from jax.sharding import PartitionSpec as P


def body(row_orbitals, column_orbitals, occupation, order, levels, times, quad_weights, freqs):
    energy = jnp.take(levels, order)
    filled = occupation.astype(jnp.float32) * 0.5
    rows_full = lax.all_to_all(row_orbitals, "tm", split_axis=0, concat_axis=1, tiled=True)
    decays = jnp.exp(-times[:, None] * energy[None, :])
    full_weight = filled[None, :] * decays
    empty_weight = (1.0 - filled)[None, :] * decays
    row_values = rows_full.astype(jnp.float32)[None]
    scaled_full = (row_values * full_weight[:, None, :]).astype(jnp.bfloat16)
    scaled_empty = (row_values * empty_weight[:, None, :]).astype(jnp.bfloat16)
    orbital_count = rows_full.shape[1]
    half_rows = scaled_full.shape[0] * scaled_full.shape[1]
    stacked = jnp.concatenate(
        (
            scaled_full.reshape(half_rows, orbital_count),
            scaled_empty.reshape(half_rows, orbital_count),
        ),
        axis=0,
    )
    col_count = column_orbitals.shape[0] * lax.axis_size("space")
    columns = lax.all_gather(column_orbitals, "tm", axis=1, tiled=True)
    greens = lax.dot_general(
        stacked,
        lax.all_gather(columns, "space", axis=0, tiled=True),
        (((1,), (1,)), ((), ())),
        preferred_element_type=jnp.float32,
    )
    product = (greens[:half_rows] * greens[half_rows:]).astype(jnp.bfloat16)
    time_count = times.shape[0]
    gathered = product.reshape(time_count, half_rows // time_count, col_count)
    sub_rows = gathered.shape[1]
    cosines = quad_weights[None, :] * jnp.cos(freqs[:, None] * times[None, :])
    spectrum = jnp.dot(
        cosines,
        gathered.reshape(time_count, sub_rows * col_count).astype(jnp.float32),
        precision=lax.Precision.HIGHEST,
    )
    return spectrum.reshape(freqs.shape[0], sub_rows, col_count)


def solution(mesh):
    placed = (P("space", "tm"), P("space", "tm"), P(), P(), P(), P(), P(), P())
    return jax.shard_map(
        body, mesh=mesh, in_specs=placed, out_specs=P(None, ("space", "tm"), None), check_vma=False
    )
```

profile of v0, /device:TPU:0, one launch (start us, length us, event | category | flops | bytes accessed | tf_op | source)
XLA Modules:
  0.0 66.5 jit_solution(772920246954484222)
XLA Ops:
  6.5 0.0 copy-start
  6.5 0.0 copy-start.1
  6.5 0.0 all-gather.2.cloned.1.call-start
  6.5 7.3 %all_gather.6 = bf16[16,2048]{1,0:T(8,128)(2,1)} all-gather(bf16[16,1024]{1,0:T(8,128)(2,1)} %param.9), channel_id=1, replica_groups=mesh['space'=16,'tm'=2] {'tm'}, dimensions={1}, use_global_device_ids=true | all-gather | bytes 98304 | tf_op jit(solution)/shard_map/all_gather | solution.py:27
  13.9 0.0 all-gather.2.cloned.1.call-update
  13.9 3.6 %all-to-all-start = ((bf16[2,256,1024]{2,1,0:T(8,128)(2,1)}), bf16[2,256,1024]{2,1,0:T(8,128)(2,1)S(1)}, u32[]{:S(2)}, u32[]{:S(2)}) async-start(bf16[2,256,1024]{2,1,0:T(8,128)(2,1)} %bitcast.18), calls=%async_computation | async-start | bytes 2097152 | tf_op jit(solution)/shard_map/all_to_all | solution.py:10
  17.5 0.0 copy-done.1
  17.5 0.0 copy-done
  17.5 0.0 copy-start.2
  17.5 0.0 copy-start.3
  17.5 11.8 %gather_fusion = f32[2048]{0:T(1024)S(1)} fusion(f32[2048]{0:T(1024)S(1)} %copy-done, s32[2048]{0:T(1024)S(1)} %fusion.7), kind=kCustom, calls=%fused_computation | custom fusion | bytes 24576 | tf_op jit(solution)/shard_map/jit(_take)/gather | solution.py:8
  29.3 0.0 copy-done.2
  29.4 0.0 copy-done.3
  29.4 0.1 fusion.6
  29.5 1.0 %all-to-all-done = bf16[2,256,1024]{2,1,0:T(8,128)(2,1)S(1)} async-done(((bf16[2,256,1024]{2,1,0:T(8,128)(2,1)}), bf16[2,256,1024]{2,1,0:T(8,128)(2,1)S(1)}, u32[]{:S(2)}, u32[]{:S(2)}) %all-to-all-start) | async-done | bytes 1048608 | tf_op jit(solution)/shard_map/all_to_all | solution.py:10
  30.5 0.2 convert_bitcast_fusion
  30.7 1.8 %copy.12 = f32[256,2,1024]{0,2,1:T(8,128)} copy(f32[256,2,1024]{2,0,1:T(8,128)S(1)} %convert_bitcast_fusion) | data formatting | bytes 4194304 | tf_op jit(solution)/shard_map/convert_element_type | solution.py:14
  32.5 1.9 %copy.13 = f32[256,2048]{1,0:T(8,128)S(1)} copy(f32[256,2048]{0,1:T(8,128)} %bitcast.14) | data formatting | bytes 4194304 | tf_op jit(solution)/shard_map/convert_element_type | solution.py:14
  34.4 3.1 %multiply_convert_fusion.1 = (bf16[2,256,2048]{2,1,0:T(8,128)(2,1)}, bf16[2,256,2048]{2,1,0:T(8,128)(2,1)}) fusion(f32[2,2048]{1,0:T(2,128)S(1)} %get-tuple-element.7, f32[256,2048]{1,0:T(8,128)S(1)} %copy.13, f32[2,2048]{1,0:T(2,128)S(1)} %get-tuple-element.8), kind=kLoop, calls=%fused_computation.6 | loop fusion | flops 4194304 | bytes 6324224 | tf_op jit(solution)/shard_map/convert_element_type | solution.py:15
  37.5 14.8 %all-gather.2.cloned.1.call-done = bf16[256,2048]{1,0:T(8,128)(2,1)} async-done(((bf16[16,2048]{1,0:T(8,128)(2,1)}), bf16[256,2048]{1,0:T(8,128)(2,1)}) %all-gather.2.cloned.1.call-update) | async-done | bytes 1048592 | tf_op jit(solution)/shard_map/all_gather | solution.py:30
  52.3 0.0 copy-start.4
  52.3 0.0 copy-start.5
  52.3 3.8 %fusion = f32[1024,256]{1,0:T(8,128)S(1)} fusion(bf16[256,2048]{1,0:T(8,128)(2,1)} %all-gather.2.cloned.1.call-done, bf16[512,2048]{1,0:T(8,128)(2,1)} %bitcast.16, bf16[512,2048]{1,0:T(8,128)(2,1)} %bitcast.15), kind=kOutput, calls=%fused_computation.1 | convolution fusion | flops 1082130432 | bytes 6291456 | tf_op jit(solution)/shard_map/dot_general | solution.py:28
  56.2 0.1 fusion.4
  56.2 0.1 reshape_reshape.3
  56.3 0.0 copy-done.4
  56.3 0.0 copy-done.5
  56.3 1.3 %fusion.8 = f32[8,256,256]{2,0,1:T(8,128)S(1)} fusion(bf16[256,256,2]{1,2,0:T(2,128)(2,1)S(1)} %bitcast.17, f32[8]{0:T(128)S(1)} %copy-done.4, f32[2]{0:T(128)S(1)} %copy-done.5, f32[2]{0:T(128)S(1)} %copy-done.3), kind=kOutput, calls=%fused_computation.18 | convolution fusion | flops 12582944 | bytes 2359344 | tf_op jit(solution)/shard_map/dot_general | solution.py:39
  57.7 2.0 %copy.14 = f32[8,256,256]{2,1,0:T(8,128)} copy(f32[8,256,256]{2,0,1:T(8,128)S(1)} %fusion.8) | data formatting | bytes 4194304 | tf_op jit(solution)/shard_map/dot_general | solution.py:39
  (3 shorter events, 0.0 us)
Async XLA Ops:
  6.5 11.0 %copy-start = (f32[2048]{0:T(1024)S(1)}, f32[2048]{0:T(1024)}, u32[]{:S(2)}) copy-start(f32[2048]{0:T(1024)} %param.12) | copy-start | bytes 24580
  6.5 10.9 %copy-start.1 = (s32[2048]{0:T(1024)S(1)}, s32[2048]{0:T(1024)}, u32[]{:S(2)}) copy-start(s32[2048]{0:T(1024)} %param.11) | copy-start | bytes 24580
  6.5 45.8 %all-gather.2.cloned.1.call-start = ((), (), s32[]{:S(2)}) async-start(), calls=%async_computation.1 | async-start | bytes 1114112 | tf_op jit(solution)/shard_map/all_gather | solution.py:30
  13.9 16.6 %all-to-all-start = ((bf16[2,256,1024]{2,1,0:T(8,128)(2,1)}), bf16[2,256,1024]{2,1,0:T(8,128)(2,1)S(1)}, u32[]{:S(2)}, u32[]{:S(2)}) async-start(bf16[2,256,1024]{2,1,0:T(8,128)(2,1)} %bitcast.18), calls=%async_computation | async-start | bytes 2097152 | tf_op jit(solution)/shard_map/all_to_all | solution.py:10
  17.5 11.8 %copy-start.2 = (s32[2048]{0:T(1024)S(1)}, s32[2048]{0:T(1024)}, u32[]{:S(2)}) copy-start(s32[2048]{0:T(1024)} %param.10) | copy-start | bytes 24580
  17.5 11.8 %copy-start.3 = (f32[2]{0:T(128)S(1)}, f32[2]{0:T(128)}, u32[]{:S(2)}) copy-start(f32[2]{0:T(128)} %param.13) | copy-start | bytes 28
  52.3 4.0 %copy-start.4 = (f32[8]{0:T(128)S(1)}, f32[8]{0:T(128)}, u32[]{:S(2)}) copy-start(f32[8]{0:T(128)} %param.15) | copy-start | bytes 100
  52.3 4.0 %copy-start.5 = (f32[2]{0:T(128)S(1)}, f32[2]{0:T(128)}, u32[]{:S(2)}) copy-start(f32[2]{0:T(128)} %param.14) | copy-start | bytes 28
Sparse Core Ops, SparseCore 0:
  14.0 38.2 all-gather.1
where the time goes:
time: 66.8 us; the launch traced here: 66.5 us
  local copies, waits for them, and re-layouts  17.6 us (26%)
  waiting for transfers between devices  15.8 us (24%)
  between operations  13.5 us (20%)
  blocking collectives  7.31 us (11%)
  matrix products  5.14 us (8%)
  starting transfers between devices  3.6 us (5%)
  other arithmetic  3.46 us (5%)
    all_gather x1, waiting for transfers between devices, body(): lax.all_gather(columns, 'space', axis=0, tiled=True)  14.8 us
    gather x1, local copies, waits for them, and re-layouts, body(): energy = jnp.take(levels, order)  11.8 us
    all_gather x1, blocking collectives, body(): columns = lax.all_gather(column_orbitals, 'tm', axis=1, tiled=True)  7.31 us
    dot_general x1, matrix products, body(): lax.dot_general(stacked, lax.all_gather(columns, 'space', axis=0, tiled=T...  3.8 us
    convert_element_type x2, local copies, waits for them, and re-layouts, body(): row_values = rows_full.astype(jnp.float32)[None]  3.73 us
    all_to_all x1, starting transfers between devices, body(): lax.all_to_all(row_orbitals, 'tm', split_axis=0, concat_axis=1, tiled=True)  3.59 us
    convert_element_type x1, other arithmetic, body(): scaled_full = (row_values * full_weight[:, None, :]).astype(jnp.bfloat16)  3.07 us
    dot_general x1, local copies, waits for them, and re-layouts, body(): jnp.dot(cosines, gathered.reshape(time_count, sub_rows * col_count).astyp...  1.96 us
  transfers between devices with their start and end apart: 2, of which 2 were waited for; matrix products, arithmetic and copies ran while one was open for 28% of the time, Pallas kernels for 0%

commit v1 on v0

v1 whole, which is shorter than its diff:
```python
import functools

import jax
import jax.numpy as jnp
from jax import lax
from jax.experimental import pallas as pl
from jax.experimental.pallas import tpu as pltpu
from jax.sharding import PartitionSpec as P


LANES = 128
MIB = 1 << 20
VMEM = pl.BlockSpec(memory_space=pltpu.VMEM)
ANY = pl.BlockSpec(memory_space=pl.ANY)


def scale_rows(read, scaled_ref, decay_ref, first_page):
    times = decay_ref.shape[0]
    block = scaled_ref.shape[0] // times
    for q in range(scaled_ref.shape[1] // LANES):
        lanes = pl.ds(q * LANES, LANES)
        values = read(lanes).astype(jnp.float32)
        for j in range(times):
            weight = decay_ref[j, pl.ds(first_page + q, 1), :]
            scaled_ref[pl.ds(j * block, block), lanes] = (values * weight).astype(jnp.bfloat16)


def own_kernel(rows_ref, levels_ref, page_ref, lane_ref, times_ref, scaled_ref, decay_ref):
    page, lane = page_ref[...], lane_ref[...]
    energy = jnp.zeros(page.shape, jnp.float32)
    for p in range(page.shape[0]):
        row = jnp.broadcast_to(levels_ref[pl.ds(p, 1), :], page.shape)
        energy = jnp.where(page == p, jnp.take_along_axis(row, lane, axis=1), energy)
    for j in range(times_ref.shape[0]):
        decay_ref[j] = jnp.exp(times_ref[pl.ds(j, 1), :] * energy)
    me = lax.axis_index("tm")
    scale_rows(lambda lanes: rows_ref[:, lanes], scaled_ref, decay_ref, me * (rows_ref.shape[1] // LANES))


def other_kernel(bits, rows_ref, decay_ref, scaled_ref):
    me = lax.axis_index("tm")
    scale_rows(lambda lanes: rows_ref[:, lanes], scaled_ref, decay_ref, (me ^ bits) * (rows_ref.shape[1] // LANES))


def half_kernel(layout, tm, far, *refs):
    pieces, refs = refs[: len(layout)], refs[len(layout) :]
    scaled, refs = refs[:tm], refs[tm:]
    occupation_ref, cosines_ref, *rest = refs
    out_ref, weights, greens, stage, sems = rest[-5:]
    block = stage.shape[1]
    width = scaled[0].shape[1]
    times = scaled[0].shape[0] // block
    columns = stage.shape[2]
    points = pieces[0].shape[-2]
    pages = width // LANES
    me = lax.axis_index("tm")
    here = lax.axis_index("space")
    peers = columns // points
    for h in range(tm):
        for q in range(pages):
            lanes = pl.ds(h * width + q * LANES, LANES)
            full = occupation_ref[pl.ds((me ^ h) * pages + q, 1), :].astype(jnp.float32) * 0.5
            empty = (1.0 - full).astype(jnp.bfloat16)
            full = full.astype(jnp.bfloat16)
            for ref, owners in zip(pieces, layout):
                for i, owner in enumerate(owners):
                    values = ref[:, lanes] if len(ref.shape) == 2 else ref[i, :, lanes]
                    start = pl.multiple_of(((here ^ owner) % peers) * points, points)
                    weights[pl.ds(start, points), lanes] = values * full
                    weights[pl.ds(columns + start, points), lanes] = values * empty

    for h in range(tm):
        part = lax.dot_general(
            scaled[h][...],
            weights[:, h * width : (h + 1) * width],
            (((1,), (1,)), ((), ())),
            preferred_element_type=jnp.float32,
        )
        greens[...] = part if h == 0 else greens[...] + part

    steps = sems.shape[0]
    rows = block // steps
    side = (here // peers) ^ far
    target = pl.ds(pl.multiple_of(side * columns, LANES), columns)
    copies = []
    for s in range(steps):
        at = pl.ds(s * rows, rows)
        polar = []
        for j in range(times):
            both = greens[pl.ds(j * block + s * rows, rows), :]
            polar.append((both[:, :columns] * both[:, columns:]).astype(jnp.bfloat16).astype(jnp.float32))
        for k in range(stage.shape[0]):
            value = cosines_ref[pl.ds(k * times, 1), :] * polar[0]
            for j in range(1, times):
                value += cosines_ref[pl.ds(k * times + j, 1), :] * polar[j]
            stage[k, at, :] = value
        copies.append(pltpu.make_async_copy(stage.at[:, at, :], out_ref.at[:, at, target], sems.at[s]))
        copies[-1].start()
    for copy in copies:
        copy.wait()


def body(row_orbitals, column_orbitals, occupation, order, levels, times, quad_weights, freqs):
    tm, space = lax.axis_size("tm"), lax.axis_size("space")
    lines = space // 4
    width = row_orbitals.shape[1]
    block = row_orbitals.shape[0] // tm
    time_count, freq_count = times.shape[0], freqs.shape[0]
    me = lax.axis_index("tm")

    def swap(value, axis, bits):
        size = lax.axis_size(axis)
        return lax.ppermute(value, axis, [(i, i ^ bits) for i in range(size)])

    halves = [column_orbitals] + [swap(column_orbitals, "tm", h) for h in range(1, tm)]
    others = [swap(lax.dynamic_slice_in_dim(row_orbitals, (me ^ h) * block, block, 0), "tm", h) for h in range(1, tm)]
    unit = jnp.concatenate(halves, axis=1)
    held = {0: unit}
    for k in range(1, lines):
        held[4 * k] = swap(unit, "space", 4 * k)
    for k in range(lines):
        held[4 * k + 2] = swap(held[4 * k], "space", 2)
    sides = [[o for o in held if o < space // 2], [o for o in held if o >= space // 2]]
    twins = [swap(jnp.stack([held[o] for o in side]), "space", 1) for side in sides]

    pages = (-1, LANES)
    small = pltpu.CompilerParams(vmem_limit_bytes=8 * MIB)
    table = (levels.shape[0] // LANES, LANES)
    own_scaled, decays = pl.pallas_call(
        own_kernel,
        out_shape=(
            jax.ShapeDtypeStruct((time_count * block, width), jnp.bfloat16),
            jax.ShapeDtypeStruct((time_count, *table), jnp.float32),
        ),
        in_specs=[VMEM] * 5,
        out_specs=(VMEM,) * 2,
        compiler_params=small,
        name="own",
    )(
        lax.dynamic_slice_in_dim(row_orbitals, me * block, block, 0),
        -levels.reshape(pages),
        (order // LANES).reshape(pages),
        (order % LANES).reshape(pages),
        jnp.broadcast_to(times[:, None], (time_count, LANES)),
    )

    scaled = [own_scaled]
    for h, rows in enumerate(others, 1):
        scaled.append(
            pl.pallas_call(
                functools.partial(other_kernel, h),
                out_shape=jax.ShapeDtypeStruct(own_scaled.shape, jnp.bfloat16),
                in_specs=[VMEM] * 2,
                out_specs=VMEM,
                compiler_params=small,
            )(rows, decays)
        )
    columns = unit.shape[0] * space // 2
    cosines = quad_weights[None, :] * jnp.cos(freqs[:, None] * times[None, :])
    cosines = jnp.broadcast_to(cosines.reshape(-1, 1), (freq_count * time_count, columns))
    steps = 4
    spectrum = []
    for i, side in enumerate(sides):
        arrays = [held[o] for o in side] + [twins[i]]
        layout = [[o] for o in side] + [[o ^ 1 for o in side]]
        count = len(arrays) + tm + 2
        spectrum = [
            pl.pallas_call(
                functools.partial(half_kernel, layout, tm, i),
                out_shape=jax.ShapeDtypeStruct((freq_count, block, 2 * columns), jnp.float32),
                in_specs=[VMEM] * count + [ANY] * len(spectrum),
                out_specs=ANY,
                scratch_shapes=[
                    pltpu.VMEM((2 * columns, tm * width), jnp.bfloat16),
                    pltpu.VMEM((time_count * block, 2 * columns), jnp.float32),
                    pltpu.VMEM((freq_count, block, columns), jnp.float32),
                    pltpu.SemaphoreType.DMA((steps,)),
                ],
                input_output_aliases={count: 0} if spectrum else {},
                compiler_params=pltpu.CompilerParams(vmem_limit_bytes=20 * MIB),
            )(*arrays, *scaled, occupation.reshape(pages), cosines, *spectrum)
        ]
    return spectrum[0]


def solution(mesh):
    placed = (P("space", "tm"), P("space", "tm"), P(), P(), P(), P(), P(), P())
    return jax.shard_map(body, mesh=mesh, in_specs=placed, out_specs=P(None, ("space", "tm"), None), check_vma=False)
```

time: 66.8 us -> 29.7 us (0.44)
  local copies, waits for them, and re-layouts: 17.6 us -> 2.31 us
  between operations: 13.5 us -> 0.14 us
  starting transfers between devices: 3.6 us -> 12.5 us
  blocking collectives: 7.31 us -> 0 us
  waiting for transfers between devices: 15.8 us -> 9.68 us
  matrix products: 5.14 us -> 0 us
  Pallas kernels: 0 us -> 4.71 us
  other arithmetic: 3.46 us -> 0.2 us
    all_gather x1 -> x0, waiting for transfers between devices: 14.8 us -> none  [body(): lax.all_gather(columns, 'space', axis=0, tiled=True)]
    ppermute x0 -> x11, starting transfers between devices: none -> 12.5 us  [swap(): return lax.ppermute(value, axis, [(i, i ^ bits) for i in range(size)])]
    gather x1 -> x0, local copies, waits for them, and re-layouts: 11.8 us -> none  [body(): energy = jnp.take(levels, order)]
    ppermute x0 -> x11, waiting for transfers between devices: none -> 9.68 us  [swap(): return lax.ppermute(value, axis, [(i, i ^ bits) for i in range(size)])]
    all_gather x1 -> x0, blocking collectives: 7.31 us -> none  [body(): columns = lax.all_gather(column_orbitals, 'tm', axis=1, tiled=True)]
    dot_general x2 -> x0, matrix products: 5.14 us -> none  [the longest x1 3.8 us: body(): lax.dot_general(stacked, lax.all_gather(columns, 'space', axis=0, tiled=T...]
    pallas_call x0 -> x4, Pallas kernels: none -> 4.71 us  [the longest x2 3.98 us: body(): pl.pallas_call(functools.partial(half_kernel, layout, tm, i), out_shape=j...]
    convert_element_type x2 -> x0, local copies, waits for them, and re-layouts: 3.73 us -> none  [body(): row_values = rows_full.astype(jnp.float32)[None]]
  transfers between devices with their start and end apart: 2 -> 11, of which waited for: 2 -> 5; matrix products, arithmetic and copies ran while one was open for 28% -> 8% of each run, Pallas kernels for 0% -> 9%
where the time goes in v1:
time: 29.7 us; the launch traced here: 29.5 us
  starting transfers between devices  12.5 us (42%)
  waiting for transfers between devices  9.68 us (33%)
  Pallas kernels  4.71 us (16%)
  local copies, waits for them, and re-layouts  2.31 us (8%)
    ppermute x11, starting transfers between devices, swap(): return lax.ppermute(value, axis, [(i, i ^ bits) for i in range(size)])  12.5 us
    ppermute x11, waiting for transfers between devices, swap(): return lax.ppermute(value, axis, [(i, i ^ bits) for i in range(size)])  9.68 us
    pallas_call x2, Pallas kernels, body(): pl.pallas_call(functools.partial(half_kernel, layout, tm, i), out_shape=j...  3.98 us
    dynamic_slice x1, local copies, waits for them, and re-layouts, body(): lax.dynamic_slice_in_dim(row_orbitals, (me ^ h) * block, block, 0)  1.27 us
    unnamed x13, local copies, waits for them, and re-layouts  0.82 us
  transfers between devices with their start and end apart: 11, of which 5 were waited for; matrix products, arithmetic and copies ran while one was open for 8% of the time, Pallas kernels for 9%

profile of v1, /device:TPU:0, one launch (start us, length us, event | category | flops | bytes accessed | tf_op | source)
XLA Modules:
  0.0 29.5 jit_solution(7813039818766164285)
XLA Ops:
  0.0 0.0 copy-start.2
  0.0 0.0 copy-start.5
  0.0 0.0 copy-start.3
  0.0 0.0 copy-start.4
  0.0 0.0 copy-start.1
  0.0 3.0 %collective-permute-start = (bf16[16,1024]{1,0:T(8,128)(2,1)}, bf16[16,1024]{1,0:T(8,128)(2,1)S(1)}, u32[]{:S(2)}, u32[]{:S(2)}) collective-permute-start(bf16[16,1024]{1,0:T(8,128)(2,1)} %param.9), channel_id=1, source_target_pairs={{0,1},{1,0},{2,3},{3,2},{4,5},{5,4},{6,7},{7,6},{8,9},{9,8},{10,11... | collective-permute-start | bytes 98312 | tf_op jit(solution)/shard_map/ppermute | solution.py:113
  3.1 0.8 %constant_dynamic-update-slice_fusion.1 = bf16[16,2048]{1,0:T(8,128)(2,1)S(1)} fusion(bf16[16,1024]{1,0:T(8,128)(2,1)} %param.9), kind=kLoop, calls=%fused_computation.13 | loop fusion | bytes 65536
  3.9 1.3 %collective-permute-done = bf16[16,1024]{1,0:T(8,128)(2,1)S(1)} collective-permute-done((bf16[16,1024]{1,0:T(8,128)(2,1)}, bf16[16,1024]{1,0:T(8,128)(2,1)S(1)}, u32[]{:S(2)}, u32[]{:S(2)}) %collective-permute-start) | collective-permute-done | bytes 32800 | tf_op jit(solution)/shard_map/ppermute | solution.py:113
  5.2 2.1 %collective-permute-start.7 = (bf16[16,2048]{1,0:T(8,128)(2,1)S(1)}, bf16[16,2048]{1,0:T(8,128)(2,1)S(1)}, u32[]{:S(2)}, u32[]{:S(2)}) collective-permute-start(bf16[16,2048]{1,0:T(8,128)(2,1)S(1)} %constant_dynamic-update-slice_fusion.refs_0_), channel_id=1, source_target_pairs={{0,8},{2,10},{4,12},{6,14},{8,0},{10,2},{12,4},{14,6},{16,24},{18,... | collective-permute-start | bytes 196616 | tf_op jit(solution)/shard_map/ppermute | solution.py:113
  7.3 1.3 %constant_dynamic-slice_fusion = (bf16[256,1024]{1,0:T(8,128)(2,1)S(1)}, bf16[256,1024]{1,0:T(8,128)(2,1)S(1)}) fusion(bf16[512,1024]{1,0:T(8,128)(2,1)} %param.8, s32[]{:T(128)S(6)} %select_n.21, s32[]{:T(128)S(6)} %select_n.18), kind=kLoop, calls=%fused_computation.16 | loop fusion | bytes 2097160 | tf_op jit(solution)/shard_map/dynamic_slice | solution.py:116
  8.5 0.0 copy-start
  8.6 1.6 %collective-permute-start.6 = (bf16[256,1024]{1,0:T(8,128)(2,1)S(1)}, bf16[256,1024]{1,0:T(8,128)(2,1)S(1)}, u32[]{:S(2)}, u32[]{:S(2)}) collective-permute-start(bf16[256,1024]{1,0:T(8,128)(2,1)S(1)} %get-tuple-element.9), channel_id=1, source_target_pairs={{0,1},{1,0},{2,3},{3,2},{4,5},{5,4},{6,7},{7,6},{8,9},{9,8},{10,11... | collective-permute-start | bytes 1572872 | tf_op jit(solution)/shard_map/ppermute | solution.py:113
  10.1 1.5 %collective-permute-start.8 = (bf16[16,2048]{1,0:T(8,128)(2,1)S(1)}, bf16[16,2048]{1,0:T(8,128)(2,1)S(1)}, u32[]{:S(2)}, u32[]{:S(2)}) collective-permute-start(bf16[16,2048]{1,0:T(8,128)(2,1)S(1)} %constant_dynamic-update-slice_fusion.refs_0_), channel_id=1, source_target_pairs={{0,4},{2,6},{4,0},{6,2},{8,12},{10,14},{12,8},{14,10},{16,20},{18,... | collective-permute-start | bytes 196616 | tf_op jit(solution)/shard_map/ppermute | solution.py:113
  11.6 2.5 %collective-permute-start.2 = (bf16[16,2048]{1,0:T(8,128)(2,1)S(1)}, bf16[16,2048]{1,0:T(8,128)(2,1)S(1)}, u32[]{:S(2)}, u32[]{:S(2)}) collective-permute-start(bf16[16,2048]{1,0:T(8,128)(2,1)S(1)} %constant_dynamic-update-slice_fusion.refs_0_), channel_id=1, source_target_pairs={{0,24},{2,26},{4,28},{6,30},{8,16},{10,18},{12,20},{14,22},{16,8},... | collective-permute-start | bytes 196616 | tf_op jit(solution)/shard_map/ppermute | solution.py:113
  14.1 0.1 collective-permute-start.1
  14.2 0.0 collective-permute-done.7.refs_1_
  14.2 0.5 %collective-permute-start.9 = (bf16[16,2048]{1,0:T(8,128)(2,1)S(1)}, bf16[16,2048]{1,0:T(8,128)(2,1)S(1)}, u32[]{:S(2)}, u32[]{:S(2)}) collective-permute-start(bf16[16,2048]{1,0:T(8,128)(2,1)S(1)} %collective-permute-done.7.refs_1_), channel_id=1, source_target_pairs={{0,4},{2,6},{4,0},{6,2},{8,12},{10,14},{12,8},{14,10},{16,20},{18,... | collective-permute-start | bytes 196616 | tf_op jit(solution)/shard_map/ppermute | solution.py:113
  14.7 0.0 copy-done.2
  14.7 3.1 %collective-permute-done.2.refs_1_ = bf16[16,2048]{1,0:T(8,128)(2,1)S(1)} collective-permute-done((bf16[16,2048]{1,0:T(8,128)(2,1)S(1)}, bf16[16,2048]{1,0:T(8,128)(2,1)S(1)}, u32[]{:S(2)}, u32[]{:S(2)}) %collective-permute-start.2) | collective-permute-done | bytes 65568 | tf_op jit(solution)/shard_map/ppermute | solution.py:113
  17.8 0.5 %collective-permute-start.4 = (bf16[16,2048]{1,0:T(8,128)(2,1)S(1)}, bf16[16,2048]{1,0:T(8,128)(2,1)S(1)}, u32[]{:S(2)}, u32[]{:S(2)}) collective-permute-start(bf16[16,2048]{1,0:T(8,128)(2,1)S(1)} %collective-permute-done.2.refs_1_), channel_id=1, source_target_pairs={{0,4},{2,6},{4,0},{6,2},{8,12},{10,14},{12,8},{14,10},{16,20},{18,... | collective-permute-start | bytes 196616 | tf_op jit(solution)/shard_map/ppermute | solution.py:113
  18.3 1.7 %collective-permute-done.1.refs_0_ = bf16[16,2048]{1,0:T(8,128)(2,1)S(1)} collective-permute-done((bf16[16,2048]{1,0:T(8,128)(2,1)S(1)}, bf16[16,2048]{1,0:T(8,128)(2,1)S(1)}, u32[]{:S(2)}, u32[]{:S(2)}) %collective-permute-start.1) | collective-permute-done | bytes 65568 | tf_op jit(solution)/shard_map/ppermute | solution.py:113
  20.0 0.5 %collective-permute-start.3 = (bf16[16,2048]{1,0:T(8,128)(2,1)S(1)}, bf16[16,2048]{1,0:T(8,128)(2,1)S(1)}, u32[]{:S(2)}, u32[]{:S(2)}) collective-permute-start(bf16[16,2048]{1,0:T(8,128)(2,1)S(1)} %collective-permute-done.1.refs_0_), channel_id=1, source_target_pairs={{0,4},{2,6},{4,0},{6,2},{8,12},{10,14},{12,8},{14,10},{16,20},{18,... | collective-permute-start | bytes 196616 | tf_op jit(solution)/shard_map/ppermute | solution.py:113
  20.5 0.0 collective-permute-done.8.refs_2_
  20.5 0.0 collective-permute-done.9.refs_3_
  20.5 0.1 collective-permute-start.10
  20.6 1.5 %collective-permute-done.4.refs_3_ = bf16[16,2048]{1,0:T(8,128)(2,1)S(1)} collective-permute-done((bf16[16,2048]{1,0:T(8,128)(2,1)S(1)}, bf16[16,2048]{1,0:T(8,128)(2,1)S(1)}, u32[]{:S(2)}, u32[]{:S(2)}) %collective-permute-start.4) | collective-permute-done | bytes 65568 | tf_op jit(solution)/shard_map/ppermute | solution.py:113
  22.1 2.2 %collective-permute-done.3.refs_2_ = bf16[16,2048]{1,0:T(8,128)(2,1)S(1)} collective-permute-done((bf16[16,2048]{1,0:T(8,128)(2,1)S(1)}, bf16[16,2048]{1,0:T(8,128)(2,1)S(1)}, u32[]{:S(2)}, u32[]{:S(2)}) %collective-permute-start.3) | collective-permute-done | bytes 65568 | tf_op jit(solution)/shard_map/ppermute | solution.py:113
  24.3 0.1 collective-permute-start.5
  24.4 0.0 copy-done.5
  24.4 0.0 copy-done.3
  24.4 0.0 copy-done.4
  24.4 0.1 cosine_multiply_fusion
  24.5 0.1 mul.46
  24.6 0.0 copy-done.1
  24.6 0.1 broadcast_in_dim.4.times_ref
  24.7 0.4 %own.1 = (bf16[512,1024]{1,0:T(8,128)(2,1)S(1)}, f32[2,16,128]{2,1,0:T(8,128)S(1)}) custom-call(bf16[256,1024]{1,0:T(8,128)(2,1)S(1)} %get-tuple-element.10.rows_ref, f32[16,128]{1,0:T(8,128)S(1)} %negate_bitcast_fusion.levels_ref, s32[16,128]{1,0:T(8,128)S(1)} %get-tuple-element.12.page_ref, s32[16,128]{1,0:T(8,128)S(1)} %get-tuple-element.11.lane_ref, ...), custom_call_target="tpu_custom_call" | custom-call | tf_op jit(solution)/shard_map/own/pallas_call | solution.py:129
  25.1 0.0 collective-permute-done.6.rows_ref
  25.1 0.3 %shard_map.82.refs_6_ = bf16[512,1024]{1,0:T(8,128)(2,1)S(1)} custom-call(bf16[256,1024]{1,0:T(8,128)(2,1)S(1)} %collective-permute-done.6.rows_ref, f32[2,16,128]{2,1,0:T(8,128)S(1)} %get-tuple-element.8.decay_ref), custom_call_target="tpu_custom_call" | custom-call | tf_op jit(solution)/shard_map/pallas_call | solution.py:150
  25.4 0.0 collective-permute-done.10.refs_4_
  25.4 0.1 broadcast_in_dim.5.refs_8_
  25.5 0.0 copy-done
  25.5 2.0 %shard_map.83.refs_9_ = f32[8,256,256]{2,1,0:T(8,128)} custom-call(bf16[16,2048]{1,0:T(8,128)(2,1)S(1)} %constant_dynamic-update-slice_fusion.refs_0_, bf16[16,2048]{1,0:T(8,128)(2,1)S(1)} %collective-permute-done.7.refs_1_, bf16[16,2048]{1,0:T(8,128)(2,1)S(1)} %collective-permute-done.8.refs_2_, bf16[16,2048]{1,0:T(8,128)(2,1)S(1)} %collective-permute-done.9.refs_3_, ...), custom_call_target="tpu_custom_call" | custom-call | tf_op jit(solution)/shard_map/pallas_call | solution.py:168
  27.5 0.0 collective-permute-done.5.refs_4_
  27.5 2.0 %shard_map.84 = f32[8,256,256]{2,1,0:T(8,128)} custom-call(bf16[16,2048]{1,0:T(8,128)(2,1)S(1)} %collective-permute-done.1.refs_0_, bf16[16,2048]{1,0:T(8,128)(2,1)S(1)} %collective-permute-done.2.refs_1_, bf16[16,2048]{1,0:T(8,128)(2,1)S(1)} %collective-permute-done.3.refs_2_, ...), custom_call_target="tpu_custom_call", output_to_operand_aliasing={{}: (9, {})} | custom-call | tf_op jit(solution)/shard_map/pallas_call | solution.py:168
  (5 shorter events, 0.1 us)
Async XLA Ops:
  0.0 14.7 %copy-start.2 = (f32[2048]{0:T(1024)S(1)}, f32[2048]{0:T(1024)}, u32[]{:S(2)}) copy-start(f32[2048]{0:T(1024)} %param.12) | copy-start | bytes 24580
  0.0 24.4 %copy-start.5 = (f32[2]{0:T(128)S(1)}, f32[2]{0:T(128)}, u32[]{:S(2)}) copy-start(f32[2]{0:T(128)} %param.13) | copy-start | bytes 28
  0.0 24.4 %copy-start.3 = (f32[8]{0:T(128)S(1)}, f32[8]{0:T(128)}, u32[]{:S(2)}) copy-start(f32[8]{0:T(128)} %param.15) | copy-start | bytes 100
  0.0 24.4 %copy-start.4 = (f32[2]{0:T(128)S(1)}, f32[2]{0:T(128)}, u32[]{:S(2)}) copy-start(f32[2]{0:T(128)} %param.14) | copy-start | bytes 28
  0.0 24.6 %copy-start.1 = (s32[2048]{0:T(1024)S(1)}, s32[2048]{0:T(1024)}, u32[]{:S(2)}) copy-start(s32[2048]{0:T(1024)} %param.11) | copy-start | bytes 24580
  0.0 5.2 %collective-permute-start = (bf16[16,1024]{1,0:T(8,128)(2,1)}, bf16[16,1024]{1,0:T(8,128)(2,1)S(1)}, u32[]{:S(2)}, u32[]{:S(2)}) collective-permute-start(bf16[16,1024]{1,0:T(8,128)(2,1)} %param.9), channel_id=1, source_target_pairs={{0,1},{1,0},{2,3},{3,2},{4,5},{5,4},{6,7},{7,6},{8,9},{9,8},{10,11... | collective-permute-start | bytes 98312 | tf_op jit(solution)/shard_map/ppermute | solution.py:113
  5.2 9.1 %collective-permute-start.7 = (bf16[16,2048]{1,0:T(8,128)(2,1)S(1)}, bf16[16,2048]{1,0:T(8,128)(2,1)S(1)}, u32[]{:S(2)}, u32[]{:S(2)}) collective-permute-start(bf16[16,2048]{1,0:T(8,128)(2,1)S(1)} %constant_dynamic-update-slice_fusion.refs_0_), channel_id=1, source_target_pairs={{0,8},{2,10},{4,12},{6,14},{8,0},{10,2},{12,4},{14,6},{16,24},{18,... | collective-permute-start | bytes 196616 | tf_op jit(solution)/shard_map/ppermute | solution.py:113
  8.5 17.0 %copy-start = (s32[2048]{0:T(1024)S(1)}, s32[2048]{0:T(1024)}, u32[]{:S(2)}) copy-start(s32[2048]{0:T(1024)} %param.10) | copy-start | bytes 24580
  8.6 16.6 %collective-permute-start.6 = (bf16[256,1024]{1,0:T(8,128)(2,1)S(1)}, bf16[256,1024]{1,0:T(8,128)(2,1)S(1)}, u32[]{:S(2)}, u32[]{:S(2)}) collective-permute-start(bf16[256,1024]{1,0:T(8,128)(2,1)S(1)} %get-tuple-element.9), channel_id=1, source_target_pairs={{0,1},{1,0},{2,3},{3,2},{4,5},{5,4},{6,7},{7,6},{8,9},{9,8},{10,11... | collective-permute-start | bytes 1572872 | tf_op jit(solution)/shard_map/ppermute | solution.py:113
  10.1 10.4 %collective-permute-start.8 = (bf16[16,2048]{1,0:T(8,128)(2,1)S(1)}, bf16[16,2048]{1,0:T(8,128)(2,1)S(1)}, u32[]{:S(2)}, u32[]{:S(2)}) collective-permute-start(bf16[16,2048]{1,0:T(8,128)(2,1)S(1)} %constant_dynamic-update-slice_fusion.refs_0_), channel_id=1, source_target_pairs={{0,4},{2,6},{4,0},{6,2},{8,12},{10,14},{12,8},{14,10},{16,20},{18,... | collective-permute-start | bytes 196616 | tf_op jit(solution)/shard_map/ppermute | solution.py:113
  11.6 6.2 %collective-permute-start.2 = (bf16[16,2048]{1,0:T(8,128)(2,1)S(1)}, bf16[16,2048]{1,0:T(8,128)(2,1)S(1)}, u32[]{:S(2)}, u32[]{:S(2)}) collective-permute-start(bf16[16,2048]{1,0:T(8,128)(2,1)S(1)} %constant_dynamic-update-slice_fusion.refs_0_), channel_id=1, source_target_pairs={{0,24},{2,26},{4,28},{6,30},{8,16},{10,18},{12,20},{14,22},{16,8},... | collective-permute-start | bytes 196616 | tf_op jit(solution)/shard_map/ppermute | solution.py:113
  14.1 5.9 %collective-permute-start.1 = (bf16[16,2048]{1,0:T(8,128)(2,1)S(1)}, bf16[16,2048]{1,0:T(8,128)(2,1)S(1)}, u32[]{:S(2)}, u32[]{:S(2)}) collective-permute-start(bf16[16,2048]{1,0:T(8,128)(2,1)S(1)} %constant_dynamic-update-slice_fusion.refs_0_), channel_id=1, source_target_pairs={{0,16},{2,18},{4,20},{6,22},{8,24},{10,26},{12,28},{14,30},{16,0},... | collective-permute-start | bytes 196616 | tf_op jit(solution)/shard_map/ppermute | solution.py:113
  14.2 6.3 %collective-permute-start.9 = (bf16[16,2048]{1,0:T(8,128)(2,1)S(1)}, bf16[16,2048]{1,0:T(8,128)(2,1)S(1)}, u32[]{:S(2)}, u32[]{:S(2)}) collective-permute-start(bf16[16,2048]{1,0:T(8,128)(2,1)S(1)} %collective-permute-done.7.refs_1_), channel_id=1, source_target_pairs={{0,4},{2,6},{4,0},{6,2},{8,12},{10,14},{12,8},{14,10},{16,20},{18,... | collective-permute-start | bytes 196616 | tf_op jit(solution)/shard_map/ppermute | solution.py:113
  17.8 4.3 %collective-permute-start.4 = (bf16[16,2048]{1,0:T(8,128)(2,1)S(1)}, bf16[16,2048]{1,0:T(8,128)(2,1)S(1)}, u32[]{:S(2)}, u32[]{:S(2)}) collective-permute-start(bf16[16,2048]{1,0:T(8,128)(2,1)S(1)} %collective-permute-done.2.refs_1_), channel_id=1, source_target_pairs={{0,4},{2,6},{4,0},{6,2},{8,12},{10,14},{12,8},{14,10},{16,20},{18,... | collective-permute-start | bytes 196616 | tf_op jit(solution)/shard_map/ppermute | solution.py:113
  20.0 4.3 %collective-permute-start.3 = (bf16[16,2048]{1,0:T(8,128)(2,1)S(1)}, bf16[16,2048]{1,0:T(8,128)(2,1)S(1)}, u32[]{:S(2)}, u32[]{:S(2)}) collective-permute-start(bf16[16,2048]{1,0:T(8,128)(2,1)S(1)} %collective-permute-done.1.refs_0_), channel_id=1, source_target_pairs={{0,4},{2,6},{4,0},{6,2},{8,12},{10,14},{12,8},{14,10},{16,20},{18,... | collective-permute-start | bytes 196616 | tf_op jit(solution)/shard_map/ppermute | solution.py:113
  20.5 4.9 %collective-permute-start.10 = (bf16[4,16,2048]{2,1,0:T(8,128)(2,1)S(1)}, bf16[4,16,2048]{2,1,0:T(8,128)(2,1)S(1)}, u32[]{:S(2)}, u32[]{:S(2)}) collective-permute-start(bf16[4,16,2048]{2,1,0:T(8,128)(2,1)S(1)} %pad_maximum_fusion.1), channel_id=1, source_target_pairs={{0,2},{2,0},{4,6},{6,4},{8,10},{10,8},{12,14},{14,12},{16,18},{18,... | collective-permute-start | bytes 786440 | tf_op jit(solution)/shard_map/ppermute | solution.py:113
  24.3 3.2 %collective-permute-start.5 = (bf16[4,16,2048]{2,1,0:T(8,128)(2,1)S(1)}, bf16[4,16,2048]{2,1,0:T(8,128)(2,1)S(1)}, u32[]{:S(2)}, u32[]{:S(2)}) collective-permute-start(bf16[4,16,2048]{2,1,0:T(8,128)(2,1)S(1)} %pad_maximum_fusion), channel_id=1, source_target_pairs={{0,2},{2,0},{4,6},{6,4},{8,10},{10,8},{12,14},{14,12},{16,18},{18,... | collective-permute-start | bytes 786440 | tf_op jit(solution)/shard_map/ppermute | solution.py:113

commit v2 on v1

v2 whole, which is shorter than its diff:
```python
import functools

import jax
import jax.numpy as jnp
from jax import lax
from jax.experimental import pallas as pl
from jax.experimental.pallas import tpu as pltpu
from jax.sharding import PartitionSpec as P


LANES = 128
STORES = 4
MIB = 1 << 20
VMEM = pl.BlockSpec(memory_space=pltpu.VMEM)
ANY = pl.BlockSpec(memory_space=pl.ANY)


def scale_rows(rows_ref, scaled_ref, decay_ref, first_page):
    block = rows_ref.shape[0]
    for q in range(scaled_ref.shape[1] // LANES):
        lanes = pl.ds(q * LANES, LANES)
        values = rows_ref[:, lanes].astype(jnp.float32)
        for j in range(decay_ref.shape[0]):
            weight = decay_ref[j, pl.ds(first_page + q, 1), :]
            scaled_ref[pl.ds(j * block, block), lanes] = (values * weight).astype(jnp.bfloat16)


def own_kernel(rows_ref, levels_ref, page_ref, lane_ref, times_ref, scaled_ref, decay_ref):
    page, lane = page_ref[...], lane_ref[...]
    energy = jnp.zeros(page.shape, jnp.float32)
    for p in range(page.shape[0]):
        row = jnp.broadcast_to(levels_ref[pl.ds(p, 1), :], page.shape)
        energy = jnp.where(page == p, jnp.take_along_axis(row, lane, axis=1), energy)
    for j in range(times_ref.shape[0]):
        decay_ref[j] = jnp.exp(times_ref[pl.ds(j, 1), :] * energy)
    me = lax.axis_index("tm")
    scale_rows(rows_ref, scaled_ref, decay_ref, me * (rows_ref.shape[1] // LANES))


def other_kernel(bits, rows_ref, decay_ref, scaled_ref):
    me = lax.axis_index("tm")
    scale_rows(rows_ref, scaled_ref, decay_ref, (me ^ bits) * (rows_ref.shape[1] // LANES))


def products(layout, tm, pieces, scaled, occupation_ref, weights, columns):
    width = scaled[0].shape[1]
    points = pieces[0].shape[-2]
    pages = width // LANES
    me = lax.axis_index("tm")
    here = lax.axis_index("space")
    for h in range(tm):
        for q in range(pages):
            lanes = pl.ds(q * LANES, LANES)
            source = pl.ds(h * width + q * LANES, LANES)
            full = occupation_ref[pl.ds((me ^ h) * pages + q, 1), :].astype(jnp.float32) * 0.5
            empty = (1.0 - full).astype(jnp.bfloat16)
            full = full.astype(jnp.bfloat16)
            for ref, owners in zip(pieces, layout):
                for i, owner in enumerate(owners):
                    values = ref[:, source] if len(ref.shape) == 2 else ref[i, :, source]
                    place = (here ^ owner ^ (h > 0)) % (columns // points)
                    start = pl.multiple_of(place * points, points)
                    weights[h][pl.ds(start, points), lanes] = values * full
                    weights[h][pl.ds(columns + start, points), lanes] = values * empty
    greens = None
    for h in range(tm):
        product = lax.dot_general(
            scaled[h][...], weights[h][...], (((1,), (1,)), ((), ())), preferred_element_type=jnp.float32
        )
        greens = product if h == 0 else greens + product
    return greens


def polar_of(greens, columns):
    return (greens[:, :columns] * greens[:, columns:]).astype(jnp.bfloat16)


def transform(read_polar, side, times, cosines_ref, out_ref, stage, sems):
    block, columns = stage.shape[1:]
    some = block // sems.shape[0]
    target = pl.ds(pl.multiple_of(side * columns, LANES), columns)
    copies = []
    for i in range(sems.shape[0]):
        at = pl.ds(i * some, some)
        polar = [read_polar(j * block + i * some, some).astype(jnp.float32) for j in range(times)]
        for k in range(stage.shape[0]):
            value = cosines_ref[pl.ds(k * times, 1), :] * polar[0]
            for j in range(1, times):
                value += cosines_ref[pl.ds(k * times + j, 1), :] * polar[j]
            stage[k, at, :] = value
        copies.append(pltpu.make_async_copy(stage.at[:, at, :], out_ref.at[:, at, target], sems.at[i]))
        copies[-1].start()
    return copies


def near_kernel(layout, tm, *refs):
    pieces, scaled = refs[: len(layout)], refs[len(layout) : len(layout) + tm]
    occupation_ref, polar_ref, *weights = refs[len(layout) + tm :]
    columns = polar_ref.shape[1]
    polar_ref[...] = polar_of(products(layout, tm, pieces, scaled, occupation_ref, weights, columns), columns)


def far_kernel(layout, tm, *refs):
    pieces, scaled = refs[: len(layout)], refs[len(layout) : len(layout) + tm]
    polar_ref, occupation_ref, cosines_ref, out_ref, *weights = refs[len(layout) + tm : -4]
    stages, sems = refs[-4:-2], refs[-2:]
    block, columns = stages[0].shape[1:]
    times = polar_ref.shape[0] // block
    space = lax.axis_size("space")
    side = lax.axis_index("space") // (space // 2)
    copies = transform(
        lambda at, size: polar_ref[pl.ds(at, size), :], side, times, cosines_ref, out_ref, stages[0], sems[0]
    )
    greens = products(layout, tm, pieces, scaled, occupation_ref, weights, columns)
    copies += transform(
        lambda at, size: polar_of(greens[at : at + size], columns),
        1 - side, times, cosines_ref, out_ref, stages[1], sems[1],
    )
    for copy in copies:
        copy.wait()


def body(row_orbitals, column_orbitals, occupation, order, levels, times, quad_weights, freqs):
    tm, space = lax.axis_size("tm"), lax.axis_size("space")
    lines = space // 4
    width = row_orbitals.shape[1]
    block = row_orbitals.shape[0] // tm
    time_count, freq_count = times.shape[0], freqs.shape[0]
    me = lax.axis_index("tm")

    def swap(value, bits, h=0):
        pairs = [(s * tm + t, (s ^ bits) * tm + (t ^ h)) for s in range(space) for t in range(tm)]
        return lax.ppermute(value, ("space", "tm"), pairs)

    halves = [column_orbitals] + [swap(column_orbitals, 1, h) for h in range(1, tm)]
    others = [swap(lax.dynamic_slice_in_dim(row_orbitals, (me ^ h) * block, block, 0), 0, h) for h in range(1, tm)]
    unit = jnp.concatenate(halves, axis=1)
    held = {0: unit}
    middle = lines // 2
    for k in range(1, middle + 1):
        held[4 * k + 1] = swap(unit, 4 * k + 1)
    base = held[4 * middle + 1]
    for k in range(1, middle):
        held[4 * (middle + k)] = swap(base, 4 * k + 1)
    for o, value in list(held.items()):
        held[o ^ 3] = swap(value, 3)
    last = list(held)[-1]
    groups = [[o for o in held if o < space // 2], [o for o in held if o >= space // 2 and o != last], [last]]
    twins = []
    for group in groups:
        stack = jnp.stack([held[o] for o in group]) if len(group) > 1 else held[group[0]]
        twins.append(swap(stack, 1))

    pages = (-1, LANES)
    small = pltpu.CompilerParams(vmem_limit_bytes=8 * MIB)
    table = (levels.shape[0] // LANES, LANES)
    own_scaled, decays = pl.pallas_call(
        own_kernel,
        out_shape=(
            jax.ShapeDtypeStruct((time_count * block, width), jnp.bfloat16),
            jax.ShapeDtypeStruct((time_count, *table), jnp.float32),
        ),
        in_specs=[VMEM] * 5,
        out_specs=(VMEM,) * 2,
        compiler_params=small,
        name="own",
    )(
        lax.dynamic_slice_in_dim(row_orbitals, me * block, block, 0),
        -levels.reshape(pages),
        (order // LANES).reshape(pages),
        (order % LANES).reshape(pages),
        jnp.broadcast_to(times[:, None], (time_count, LANES)),
    )

    scaled = [own_scaled]
    for h, rows in enumerate(others, 1):
        scaled.append(
            pl.pallas_call(
                functools.partial(other_kernel, h),
                out_shape=jax.ShapeDtypeStruct(own_scaled.shape, jnp.bfloat16),
                in_specs=[VMEM] * 2,
                out_specs=VMEM,
                compiler_params=small,
            )(rows, decays)
        )
    columns = unit.shape[0] * space // 2
    cosines = quad_weights[None, :] * jnp.cos(freqs[:, None] * times[None, :])
    cosines = jnp.broadcast_to(cosines.reshape(-1, 1), (freq_count * time_count, columns))
    layouts, arrays = [], []
    for side in (0, 1):
        mine = [i for i in range(len(groups)) if (i > 0) == side]
        layouts.append([[o] for i in mine for o in groups[i]] + [[o ^ 1 for o in groups[i]] for i in mine])
        arrays.append([held[o] for i in mine for o in groups[i]] + [twins[i] for i in mine])
    weights = [pltpu.VMEM((2 * columns, width), jnp.bfloat16)] * tm
    stage = pltpu.VMEM((freq_count, block, columns), jnp.float32)
    staging = [stage, stage, pltpu.SemaphoreType.DMA((2,)), pltpu.SemaphoreType.DMA((STORES,))]
    result = jax.ShapeDtypeStruct((freq_count, block, 2 * columns), jnp.float32)
    large = pltpu.CompilerParams(vmem_limit_bytes=20 * MIB)
    occupation = occupation.reshape(pages)
    polar = pl.pallas_call(
        functools.partial(near_kernel, layouts[0], tm),
        out_shape=jax.ShapeDtypeStruct((time_count * block, columns), jnp.bfloat16),
        in_specs=[VMEM] * (len(arrays[0]) + tm + 1),
        out_specs=VMEM,
        scratch_shapes=weights,
        compiler_params=large,
        name="near",
    )(*arrays[0], *scaled, occupation)
    return pl.pallas_call(
        functools.partial(far_kernel, layouts[1], tm),
        out_shape=result,
        in_specs=[VMEM] * (len(arrays[1]) + tm + 3),
        out_specs=ANY,
        scratch_shapes=weights + staging,
        compiler_params=large,
        name="far",
    )(*arrays[1], *scaled, polar, occupation, cosines)


def solution(mesh):
    placed = (P("space", "tm"), P("space", "tm"), P(), P(), P(), P(), P(), P())
    return jax.shard_map(body, mesh=mesh, in_specs=placed, out_specs=P(None, ("space", "tm"), None), check_vma=False)
```

time: 29.7 us -> 27.4 us (0.923)
  Pallas kernels: 4.71 us -> 3.83 us
  local copies, waits for them, and re-layouts: 2.31 us -> 1.52 us
  waiting for transfers between devices: 9.68 us -> 9.12 us
    pallas_call x2, Pallas kernels: 3.98 us -> 3.09 us  [the longest x1 2.09 us: body(): pl.pallas_call(functools.partial(far_kernel, layouts[1], tm), out_shape=r...]
    unnamed x13 -> x15, local copies, waits for them, and re-layouts: 0.82 us -> 0.03 us
    ppermute x11 -> x12, waiting for transfers between devices: 9.68 us -> 9.12 us  [swap(): return lax.ppermute(value, ('space', 'tm'), pairs)]
    ppermute x11 -> x12, starting transfers between devices: 12.5 us -> 12.5 us  [swap(): return lax.ppermute(value, ('space', 'tm'), pairs)]
  transfers between devices with their start and end apart: 11 -> 12, of which waited for: 5 -> 4; matrix products, arithmetic and copies ran while one was open for 8% -> 6% of each run, Pallas kernels for 9% -> 6%
where the time goes in v2:
time: 27.4 us; the launch traced here: 27.2 us
  starting transfers between devices  12.5 us (46%)
  waiting for transfers between devices  9.12 us (33%)
  Pallas kernels  3.83 us (14%)
  local copies, waits for them, and re-layouts  1.52 us (6%)
    ppermute x12, starting transfers between devices, swap(): return lax.ppermute(value, ('space', 'tm'), pairs)  12.5 us
    ppermute x12, waiting for transfers between devices, swap(): return lax.ppermute(value, ('space', 'tm'), pairs)  9.12 us
    pallas_call x1, Pallas kernels, body(): pl.pallas_call(functools.partial(far_kernel, layouts[1], tm), out_shape=r...  2.09 us
    dynamic_slice x1, local copies, waits for them, and re-layouts, body(): lax.dynamic_slice_in_dim(row_orbitals, (me ^ h) * block, block, 0)  1.27 us
    pallas_call x1, Pallas kernels, body(): pl.pallas_call(functools.partial(near_kernel, layouts[0], tm), out_shape=...  1.01 us
  transfers between devices with their start and end apart: 12, of which 4 were waited for; matrix products, arithmetic and copies ran while one was open for 6% of the time, Pallas kernels for 6%

profile of v2, /device:TPU:0, one launch (start us, length us, event | category | flops | bytes accessed | tf_op | source)
XLA Modules:
  0.0 27.2 jit_solution(11921430216877280037)
XLA Ops:
  0.0 0.0 copy-start.1
  0.0 0.0 copy-start.2
  0.0 0.0 copy-start.3
  0.0 0.0 copy-start.6
  0.0 0.0 copy-start.4
  0.0 0.0 copy-start.5
  0.0 2.5 %collective-permute-start = (bf16[16,1024]{1,0:T(8,128)(2,1)}, bf16[16,1024]{1,0:T(8,128)(2,1)S(1)}, u32[]{:S(2)}, u32[]{:S(2)}) collective-permute-start(bf16[16,1024]{1,0:T(8,128)(2,1)} %param.9), channel_id=1, source_target_pairs={{0,3},{1,2},{2,1},{3,0},{4,7},{5,6},{6,5},{7,4},{8,11},{9,10},{10,... | collective-permute-start | bytes 98312 | tf_op jit(solution)/shard_map/ppermute | solution.py:133
  2.5 1.3 %constant_dynamic-slice_fusion = (bf16[256,1024]{1,0:T(8,128)(2,1)S(1)}, bf16[256,1024]{1,0:T(8,128)(2,1)S(1)}) fusion(bf16[512,1024]{1,0:T(8,128)(2,1)} %param.8, s32[]{:T(128)S(6)} %select_n.21, s32[]{:T(128)S(6)} %select_n.18), kind=kLoop, calls=%fused_computation.16 | loop fusion | bytes 2097160 | tf_op jit(solution)/shard_map/dynamic_slice | solution.py:136
  3.8 0.0 copy-start
  3.8 0.7 %collective-permute-start.7 = (bf16[256,1024]{1,0:T(8,128)(2,1)S(1)}, bf16[256,1024]{1,0:T(8,128)(2,1)S(1)}, u32[]{:S(2)}, u32[]{:S(2)}) collective-permute-start(bf16[256,1024]{1,0:T(8,128)(2,1)S(1)} %get-tuple-element.9), channel_id=1, source_target_pairs={{0,1},{1,0},{2,3},{3,2},{4,5},{5,4},{6,7},{7,6},{8,9},{9,8},{10,11... | collective-permute-start | bytes 1572872 | tf_op jit(solution)/shard_map/ppermute | solution.py:133
  4.4 0.0 copy-done.1
  4.5 0.1 collective-permute-done
  4.6 2.1 %collective-permute-start.8 = (bf16[16,2048]{1,0:T(8,128)(2,1)S(1)}, bf16[16,2048]{1,0:T(8,128)(2,1)S(1)}, u32[]{:S(2)}, u32[]{:S(2)}) collective-permute-start(bf16[16,2048]{1,0:T(8,128)(2,1)S(1)} %constant_dynamic-update-slice_fusion.refs_0_), channel_id=1, source_target_pairs={{0,10},{1,11},{2,8},{3,9},{4,14},{5,15},{6,12},{7,13},{8,2},{9,3},... | collective-permute-start | bytes 196616 | tf_op jit(solution)/shard_map/ppermute | solution.py:133
  6.7 0.0 copy-done.2
  6.8 1.6 %collective-permute-start.9 = (bf16[16,2048]{1,0:T(8,128)(2,1)S(1)}, bf16[16,2048]{1,0:T(8,128)(2,1)S(1)}, u32[]{:S(2)}, u32[]{:S(2)}) collective-permute-start(bf16[16,2048]{1,0:T(8,128)(2,1)S(1)} %constant_dynamic-update-slice_fusion.refs_0_), channel_id=1, source_target_pairs={{0,6},{1,7},{2,4},{3,5},{4,2},{5,3},{6,0},{7,1},{8,14},{9,15},{10,... | collective-permute-start | bytes 196616 | tf_op jit(solution)/shard_map/ppermute | solution.py:133
  8.3 2.3 %collective-permute-start.1 = (bf16[16,2048]{1,0:T(8,128)(2,1)S(1)}, bf16[16,2048]{1,0:T(8,128)(2,1)S(1)}, u32[]{:S(2)}, u32[]{:S(2)}) collective-permute-start(bf16[16,2048]{1,0:T(8,128)(2,1)S(1)} %constant_dynamic-update-slice_fusion.refs_0_), channel_id=1, source_target_pairs={{0,18},{1,19},{2,16},{3,17},{4,22},{5,23},{6,20},{7,21},{8,26},{9,... | collective-permute-start | bytes 196616 | tf_op jit(solution)/shard_map/ppermute | solution.py:133
  10.6 0.0 collective-permute-done.8.refs_1_
  10.6 0.5 %collective-permute-start.10 = (bf16[16,2048]{1,0:T(8,128)(2,1)S(1)}, bf16[16,2048]{1,0:T(8,128)(2,1)S(1)}, u32[]{:S(2)}, u32[]{:S(2)}) collective-permute-start(bf16[16,2048]{1,0:T(8,128)(2,1)S(1)} %collective-permute-done.8.refs_1_), channel_id=1, source_target_pairs={{0,6},{1,7},{2,4},{3,5},{4,2},{5,3},{6,0},{7,1},{8,14},{9,15},{10,... | collective-permute-start | bytes 196616 | tf_op jit(solution)/shard_map/ppermute | solution.py:133
  11.2 0.0 copy-done.3
  11.2 3.7 %collective-permute-done.1.refs_0_ = bf16[16,2048]{1,0:T(8,128)(2,1)S(1)} collective-permute-done((bf16[16,2048]{1,0:T(8,128)(2,1)S(1)}, bf16[16,2048]{1,0:T(8,128)(2,1)S(1)}, u32[]{:S(2)}, u32[]{:S(2)}) %collective-permute-start.1) | collective-permute-done | bytes 65568 | tf_op jit(solution)/shard_map/ppermute | solution.py:133
  14.9 0.1 collective-permute-start.3
  15.0 0.0 collective-permute-start.2
  15.0 0.0 collective-permute-done.9.refs_2_
  15.0 0.0 collective-permute-done.10.refs_3_
  15.0 0.5 %collective-permute-start.11 = (bf16[4,16,2048]{2,1,0:T(8,128)(2,1)S(1)}, bf16[4,16,2048]{2,1,0:T(8,128)(2,1)S(1)}, u32[]{:S(2)}, u32[]{:S(2)}) collective-permute-start(bf16[4,16,2048]{2,1,0:T(8,128)(2,1)S(1)} %pad_maximum_fusion), channel_id=1, source_target_pairs={{0,2},{1,3},{2,0},{3,1},{4,6},{5,7},{6,4},{7,5},{8,10},{9,11},{10,... | collective-permute-start | bytes 786440 | tf_op jit(solution)/shard_map/ppermute | solution.py:133
  15.5 3.3 %collective-permute-done.2.refs_1_ = bf16[16,2048]{1,0:T(8,128)(2,1)S(1)} collective-permute-done((bf16[16,2048]{1,0:T(8,128)(2,1)S(1)}, bf16[16,2048]{1,0:T(8,128)(2,1)S(1)}, u32[]{:S(2)}, u32[]{:S(2)}) %collective-permute-start.2) | collective-permute-done | bytes 65568 | tf_op jit(solution)/shard_map/ppermute | solution.py:133
  18.8 1.7 %collective-permute-start.4 = (bf16[16,2048]{1,0:T(8,128)(2,1)S(1)}, bf16[16,2048]{1,0:T(8,128)(2,1)S(1)}, u32[]{:S(2)}, u32[]{:S(2)}) collective-permute-start(bf16[16,2048]{1,0:T(8,128)(2,1)S(1)} %collective-permute-done.2.refs_1_), channel_id=1, source_target_pairs={{0,6},{1,7},{2,4},{3,5},{4,2},{5,3},{6,0},{7,1},{8,14},{9,15},{10,... | collective-permute-start | bytes 196616 | tf_op jit(solution)/shard_map/ppermute | solution.py:133
  20.5 0.0 collective-permute-done.3.refs_2_
  20.5 0.2 collective-permute-start.5
  20.7 1.9 %collective-permute-done.4.refs_3_ = bf16[16,2048]{1,0:T(8,128)(2,1)S(1)} collective-permute-done((bf16[16,2048]{1,0:T(8,128)(2,1)S(1)}, bf16[16,2048]{1,0:T(8,128)(2,1)S(1)}, u32[]{:S(2)}, u32[]{:S(2)}) %collective-permute-start.4) | collective-permute-done | bytes 65568 | tf_op jit(solution)/shard_map/ppermute | solution.py:133
  22.6 0.4 %collective-permute-start.6 = (bf16[16,2048]{1,0:T(8,128)(2,1)S(1)}, bf16[16,2048]{1,0:T(8,128)(2,1)S(1)}, u32[]{:S(2)}, u32[]{:S(2)}) collective-permute-start(bf16[16,2048]{1,0:T(8,128)(2,1)S(1)} %collective-permute-done.4.refs_3_), channel_id=1, source_target_pairs={{0,2},{1,3},{2,0},{3,1},{4,6},{5,7},{6,4},{7,5},{8,10},{9,11},{10,... | collective-permute-start | bytes 196616 | tf_op jit(solution)/shard_map/ppermute | solution.py:133
  23.0 0.0 copy-done.6
  23.0 0.0 copy-done.4
  23.0 0.0 copy-done.5
  23.0 0.1 cosine_multiply_fusion
  23.1 0.1 mul.46
  23.2 0.1 broadcast_in_dim.4.times_ref
  23.3 0.4 %own.1 = (bf16[512,1024]{1,0:T(8,128)(2,1)S(1)}, f32[2,16,128]{2,1,0:T(8,128)S(1)}) custom-call(bf16[256,1024]{1,0:T(8,128)(2,1)S(1)} %get-tuple-element.10.rows_ref, f32[16,128]{1,0:T(8,128)S(1)} %negate_bitcast_fusion.levels_ref, s32[16,128]{1,0:T(8,128)S(1)} %get-tuple-element.12.page_ref, s32[16,128]{1,0:T(8,128)S(1)} %get-tuple-element.11.lane_ref, ...), custom_call_target="tpu_custom_call" | custom-call | tf_op jit(solution)/shard_map/own/pallas_call | solution.py:157
  23.7 0.0 collective-permute-done.7.rows_ref
  23.7 0.3 %shard_map.82.refs_6_.refs_7_ = bf16[512,1024]{1,0:T(8,128)(2,1)S(1)} custom-call(bf16[256,1024]{1,0:T(8,128)(2,1)S(1)} %collective-permute-done.7.rows_ref, f32[2,16,128]{2,1,0:T(8,128)S(1)} %get-tuple-element.8.decay_ref), custom_call_target="tpu_custom_call" | custom-call | tf_op jit(solution)/shard_map/pallas_call | solution.py:178
  24.0 0.0 collective-permute-done.11.refs_4_
  24.0 0.0 copy-done
  24.1 1.0 %near.1.refs_8_ = bf16[512,128]{1,0:T(8,128)(2,1)S(1)} custom-call(bf16[16,2048]{1,0:T(8,128)(2,1)S(1)} %constant_dynamic-update-slice_fusion.refs_0_, bf16[16,2048]{1,0:T(8,128)(2,1)S(1)} %collective-permute-done.8.refs_1_, bf16[16,2048]{1,0:T(8,128)(2,1)S(1)} %collective-permute-done.9.refs_2_, bf16[16,2048]{1,0:T(8,128)(2,1)S(1)} %collective-permute-done.10.refs_3_, ...), custom_call_target="tpu_custom_call" | custom-call | tf_op jit(solution)/shard_map/near/pallas_call | solution.py:200
  25.1 0.0 collective-permute-done.6.refs_5_
  25.1 0.0 collective-permute-done.5.refs_4_
  25.1 0.1 broadcast_in_dim.5.refs_10_
  25.2 2.1 %far.1 = f32[8,256,256]{2,1,0:T(8,128)} custom-call(bf16[16,2048]{1,0:T(8,128)(2,1)S(1)} %collective-permute-done.1.refs_0_, bf16[16,2048]{1,0:T(8,128)(2,1)S(1)} %collective-permute-done.2.refs_1_, bf16[16,2048]{1,0:T(8,128)(2,1)S(1)} %collective-permute-done.3.refs_2_, bf16[16,2048]{1,0:T(8,128)(2,1)S(1)} %collective-permute-done.4.refs_3_, ...), custom_call_target="tpu_custom_call" | custom-call | tf_op jit(solution)/shard_map/far/pallas_call | solution.py:209
  (6 shorter events, 0.1 us)
Async XLA Ops:
  0.0 4.5 %copy-start.1 = (bf16[16,1024]{1,0:T(8,128)(2,1)S(1)}, bf16[16,1024]{1,0:T(8,128)(2,1)}, u32[]{:S(2)}) copy-start(bf16[16,1024]{1,0:T(8,128)(2,1)} %param.9) | copy-start | bytes 98308
  0.0 6.7 %copy-start.2 = (s32[2048]{0:T(1024)S(1)}, s32[2048]{0:T(1024)}, u32[]{:S(2)}) copy-start(s32[2048]{0:T(1024)} %param.11) | copy-start | bytes 24580
  0.0 11.2 %copy-start.3 = (f32[2048]{0:T(1024)S(1)}, f32[2048]{0:T(1024)}, u32[]{:S(2)}) copy-start(f32[2048]{0:T(1024)} %param.12) | copy-start | bytes 24580
  0.0 23.0 %copy-start.6 = (f32[2]{0:T(128)S(1)}, f32[2]{0:T(128)}, u32[]{:S(2)}) copy-start(f32[2]{0:T(128)} %param.13) | copy-start | bytes 28
  0.0 23.0 %copy-start.4 = (f32[8]{0:T(128)S(1)}, f32[8]{0:T(128)}, u32[]{:S(2)}) copy-start(f32[8]{0:T(128)} %param.15) | copy-start | bytes 100
  0.0 23.0 %copy-start.5 = (f32[2]{0:T(128)S(1)}, f32[2]{0:T(128)}, u32[]{:S(2)}) copy-start(f32[2]{0:T(128)} %param.14) | copy-start | bytes 28
  0.0 4.6 %collective-permute-start = (bf16[16,1024]{1,0:T(8,128)(2,1)}, bf16[16,1024]{1,0:T(8,128)(2,1)S(1)}, u32[]{:S(2)}, u32[]{:S(2)}) collective-permute-start(bf16[16,1024]{1,0:T(8,128)(2,1)} %param.9), channel_id=1, source_target_pairs={{0,3},{1,2},{2,1},{3,0},{4,7},{5,6},{6,5},{7,4},{8,11},{9,10},{10,... | collective-permute-start | bytes 98312 | tf_op jit(solution)/shard_map/ppermute | solution.py:133
  3.8 20.3 %copy-start = (s32[2048]{0:T(1024)S(1)}, s32[2048]{0:T(1024)}, u32[]{:S(2)}) copy-start(s32[2048]{0:T(1024)} %param.10) | copy-start | bytes 24580
  3.8 19.9 %collective-permute-start.7 = (bf16[256,1024]{1,0:T(8,128)(2,1)S(1)}, bf16[256,1024]{1,0:T(8,128)(2,1)S(1)}, u32[]{:S(2)}, u32[]{:S(2)}) collective-permute-start(bf16[256,1024]{1,0:T(8,128)(2,1)S(1)} %get-tuple-element.9), channel_id=1, source_target_pairs={{0,1},{1,0},{2,3},{3,2},{4,5},{5,4},{6,7},{7,6},{8,9},{9,8},{10,11... | collective-permute-start | bytes 1572872 | tf_op jit(solution)/shard_map/ppermute | solution.py:133
  4.6 6.0 %collective-permute-start.8 = (bf16[16,2048]{1,0:T(8,128)(2,1)S(1)}, bf16[16,2048]{1,0:T(8,128)(2,1)S(1)}, u32[]{:S(2)}, u32[]{:S(2)}) collective-permute-start(bf16[16,2048]{1,0:T(8,128)(2,1)S(1)} %constant_dynamic-update-slice_fusion.refs_0_), channel_id=1, source_target_pairs={{0,10},{1,11},{2,8},{3,9},{4,14},{5,15},{6,12},{7,13},{8,2},{9,3},... | collective-permute-start | bytes 196616 | tf_op jit(solution)/shard_map/ppermute | solution.py:133
  6.8 8.2 %collective-permute-start.9 = (bf16[16,2048]{1,0:T(8,128)(2,1)S(1)}, bf16[16,2048]{1,0:T(8,128)(2,1)S(1)}, u32[]{:S(2)}, u32[]{:S(2)}) collective-permute-start(bf16[16,2048]{1,0:T(8,128)(2,1)S(1)} %constant_dynamic-update-slice_fusion.refs_0_), channel_id=1, source_target_pairs={{0,6},{1,7},{2,4},{3,5},{4,2},{5,3},{6,0},{7,1},{8,14},{9,15},{10,... | collective-permute-start | bytes 196616 | tf_op jit(solution)/shard_map/ppermute | solution.py:133
  8.3 6.6 %collective-permute-start.1 = (bf16[16,2048]{1,0:T(8,128)(2,1)S(1)}, bf16[16,2048]{1,0:T(8,128)(2,1)S(1)}, u32[]{:S(2)}, u32[]{:S(2)}) collective-permute-start(bf16[16,2048]{1,0:T(8,128)(2,1)S(1)} %constant_dynamic-update-slice_fusion.refs_0_), channel_id=1, source_target_pairs={{0,18},{1,19},{2,16},{3,17},{4,22},{5,23},{6,20},{7,21},{8,26},{9,... | collective-permute-start | bytes 196616 | tf_op jit(solution)/shard_map/ppermute | solution.py:133
  10.6 4.3 %collective-permute-start.10 = (bf16[16,2048]{1,0:T(8,128)(2,1)S(1)}, bf16[16,2048]{1,0:T(8,128)(2,1)S(1)}, u32[]{:S(2)}, u32[]{:S(2)}) collective-permute-start(bf16[16,2048]{1,0:T(8,128)(2,1)S(1)} %collective-permute-done.8.refs_1_), channel_id=1, source_target_pairs={{0,6},{1,7},{2,4},{3,5},{4,2},{5,3},{6,0},{7,1},{8,14},{9,15},{10,... | collective-permute-start | bytes 196616 | tf_op jit(solution)/shard_map/ppermute | solution.py:133
  14.9 5.6 %collective-permute-start.3 = (bf16[16,2048]{1,0:T(8,128)(2,1)S(1)}, bf16[16,2048]{1,0:T(8,128)(2,1)S(1)}, u32[]{:S(2)}, u32[]{:S(2)}) collective-permute-start(bf16[16,2048]{1,0:T(8,128)(2,1)S(1)} %collective-permute-done.1.refs_0_), channel_id=1, source_target_pairs={{0,6},{1,7},{2,4},{3,5},{4,2},{5,3},{6,0},{7,1},{8,14},{9,15},{10,... | collective-permute-start | bytes 196616 | tf_op jit(solution)/shard_map/ppermute | solution.py:133
  15.0 3.8 %collective-permute-start.2 = (bf16[16,2048]{1,0:T(8,128)(2,1)S(1)}, bf16[16,2048]{1,0:T(8,128)(2,1)S(1)}, u32[]{:S(2)}, u32[]{:S(2)}) collective-permute-start(bf16[16,2048]{1,0:T(8,128)(2,1)S(1)} %collective-permute-done.1.refs_0_), channel_id=1, source_target_pairs={{0,10},{1,11},{2,8},{3,9},{4,14},{5,15},{6,12},{7,13},{8,2},{9,3},... | collective-permute-start | bytes 196616 | tf_op jit(solution)/shard_map/ppermute | solution.py:133
  15.0 9.0 %collective-permute-start.11 = (bf16[4,16,2048]{2,1,0:T(8,128)(2,1)S(1)}, bf16[4,16,2048]{2,1,0:T(8,128)(2,1)S(1)}, u32[]{:S(2)}, u32[]{:S(2)}) collective-permute-start(bf16[4,16,2048]{2,1,0:T(8,128)(2,1)S(1)} %pad_maximum_fusion), channel_id=1, source_target_pairs={{0,2},{1,3},{2,0},{3,1},{4,6},{5,7},{6,4},{7,5},{8,10},{9,11},{10,... | collective-permute-start | bytes 786440 | tf_op jit(solution)/shard_map/ppermute | solution.py:133
  18.8 3.8 %collective-permute-start.4 = (bf16[16,2048]{1,0:T(8,128)(2,1)S(1)}, bf16[16,2048]{1,0:T(8,128)(2,1)S(1)}, u32[]{:S(2)}, u32[]{:S(2)}) collective-permute-start(bf16[16,2048]{1,0:T(8,128)(2,1)S(1)} %collective-permute-done.2.refs_1_), channel_id=1, source_target_pairs={{0,6},{1,7},{2,4},{3,5},{4,2},{5,3},{6,0},{7,1},{8,14},{9,15},{10,... | collective-permute-start | bytes 196616 | tf_op jit(solution)/shard_map/ppermute | solution.py:133
  20.5 4.6 %collective-permute-start.5 = (bf16[3,16,2048]{2,1,0:T(8,128)(2,1)S(1)}, bf16[3,16,2048]{2,1,0:T(8,128)(2,1)S(1)}, u32[]{:S(2)}, u32[]{:S(2)}) collective-permute-start(bf16[3,16,2048]{2,1,0:T(8,128)(2,1)S(1)} %pad_maximum_fusion.1), channel_id=1, source_target_pairs={{0,2},{1,3},{2,0},{3,1},{4,6},{5,7},{6,4},{7,5},{8,10},{9,11},{10,... | collective-permute-start | bytes 589832 | tf_op jit(solution)/shard_map/ppermute | solution.py:133
  22.6 2.5 %collective-permute-start.6 = (bf16[16,2048]{1,0:T(8,128)(2,1)S(1)}, bf16[16,2048]{1,0:T(8,128)(2,1)S(1)}, u32[]{:S(2)}, u32[]{:S(2)}) collective-permute-start(bf16[16,2048]{1,0:T(8,128)(2,1)S(1)} %collective-permute-done.4.refs_3_), channel_id=1, source_target_pairs={{0,2},{1,3},{2,0},{3,1},{4,6},{5,7},{6,4},{7,5},{8,10},{9,11},{10,... | collective-permute-start | bytes 196616 | tf_op jit(solution)/shard_map/ppermute | solution.py:133

commit v3 on v2

--- a/solution.py
+++ b/solution.py
@@ -48,6 +48,7 @@
     pages = width // LANES
     me = lax.axis_index("tm")
     here = lax.axis_index("space")
+    greens = None
     for h in range(tm):
         for q in range(pages):
             lanes = pl.ds(q * LANES, LANES)
@@ -62,8 +63,6 @@
                     start = pl.multiple_of(place * points, points)
                     weights[h][pl.ds(start, points), lanes] = values * full
                     weights[h][pl.ds(columns + start, points), lanes] = values * empty
-    greens = None
-    for h in range(tm):
         product = lax.dot_general(
             scaled[h][...], weights[h][...], (((1,), (1,)), ((), ())), preferred_element_type=jnp.float32
         )
@@ -75,47 +74,48 @@
     return (greens[:, :columns] * greens[:, columns:]).astype(jnp.bfloat16)
 
 
-def transform(read_polar, side, times, cosines_ref, out_ref, stage, sems):
-    block, columns = stage.shape[1:]
-    some = block // sems.shape[0]
-    target = pl.ds(pl.multiple_of(side * columns, LANES), columns)
-    copies = []
-    for i in range(sems.shape[0]):
-        at = pl.ds(i * some, some)
-        polar = [read_polar(j * block + i * some, some).astype(jnp.float32) for j in range(times)]
-        for k in range(stage.shape[0]):
-            value = cosines_ref[pl.ds(k * times, 1), :] * polar[0]
-            for j in range(1, times):
-                value += cosines_ref[pl.ds(k * times + j, 1), :] * polar[j]
-            stage[k, at, :] = value
-        copies.append(pltpu.make_async_copy(stage.at[:, at, :], out_ref.at[:, at, target], sems.at[i]))
-        copies[-1].start()
-    return copies
+def transform(read_polar, times, cosines_ref, stage, at, some):
+    block = stage.shape[1]
+    polar = [read_polar(j * block + at, some).astype(jnp.float32) for j in range(times)]
+    for k in range(stage.shape[0]):
+        value = cosines_ref[pl.ds(k * times, 1), :] * polar[0]
+        for j in range(1, times):
+            value += cosines_ref[pl.ds(k * times + j, 1), :] * polar[j]
+        stage[k, pl.ds(at, some), :] = value
 
 
 def near_kernel(layout, tm, *refs):
     pieces, scaled = refs[: len(layout)], refs[len(layout) : len(layout) + tm]
-    occupation_ref, polar_ref, *weights = refs[len(layout) + tm :]
-    columns = polar_ref.shape[1]
-    polar_ref[...] = polar_of(products(layout, tm, pieces, scaled, occupation_ref, weights, columns), columns)
+    occupation_ref, cosines_ref, stage, *weights = refs[len(layout) + tm :]
+    block, columns = stage.shape[1:]
+    greens = products(layout, tm, pieces, scaled, occupation_ref, weights, columns)
+    times = greens.shape[0] // block
+    transform(lambda at, size: polar_of(greens[at : at + size], columns), times, cosines_ref, stage, 0, block)
 
 
 def far_kernel(layout, tm, *refs):
     pieces, scaled = refs[: len(layout)], refs[len(layout) : len(layout) + tm]
-    polar_ref, occupation_ref, cosines_ref, out_ref, *weights = refs[len(layout) + tm : -4]
-    stages, sems = refs[-4:-2], refs[-2:]
-    block, columns = stages[0].shape[1:]
-    times = polar_ref.shape[0] // block
+    near_ref, occupation_ref, cosines_ref, out_ref, *weights = refs[len(layout) + tm : -3]
+    stage, near_sem, sems = refs[-3:]
+    block, columns = stage.shape[1:]
     space = lax.axis_size("space")
     side = lax.axis_index("space") // (space // 2)
-    copies = transform(
-        lambda at, size: polar_ref[pl.ds(at, size), :], side, times, cosines_ref, out_ref, stages[0], sems[0]
-    )
+
+    def target(which):
+        return pl.ds(pl.multiple_of(which * columns, LANES), columns)
+
+    copies = [pltpu.make_async_copy(near_ref, out_ref.at[:, :, target(side)], near_sem)]
+    copies[0].start()
     greens = products(layout, tm, pieces, scaled, occupation_ref, weights, columns)
-    copies += transform(
-        lambda at, size: polar_of(greens[at : at + size], columns),
-        1 - side, times, cosines_ref, out_ref, stages[1], sems[1],
-    )
+    times = greens.shape[0] // block
+    some = block // sems.shape[0]
+    for i in range(sems.shape[0]):
+        transform(
+            lambda at, size: polar_of(greens[at : at + size], columns), times, cosines_ref, stage, i * some, some
+        )
+        rows = pl.ds(i * some, some)
+        copies.append(pltpu.make_async_copy(stage.at[:, rows, :], out_ref.at[:, rows, target(1 - side)], sems.at[i]))
+        copies[-1].start()
     for copy in copies:
         copy.wait()
 
@@ -192,20 +192,23 @@
         layouts.append([[o] for i in mine for o in groups[i]] + [[o ^ 1 for o in groups[i]] for i in mine])
         arrays.append([held[o] for i in mine for o in groups[i]] + [twins[i] for i in mine])
     weights = [pltpu.VMEM((2 * columns, width), jnp.bfloat16)] * tm
-    stage = pltpu.VMEM((freq_count, block, columns), jnp.float32)
-    staging = [stage, stage, pltpu.SemaphoreType.DMA((2,)), pltpu.SemaphoreType.DMA((STORES,))]
+    staging = [
+        pltpu.VMEM((freq_count, block, columns), jnp.float32),
+        pltpu.SemaphoreType.DMA,
+        pltpu.SemaphoreType.DMA((STORES,)),
+    ]
     result = jax.ShapeDtypeStruct((freq_count, block, 2 * columns), jnp.float32)
     large = pltpu.CompilerParams(vmem_limit_bytes=20 * MIB)
     occupation = occupation.reshape(pages)
-    polar = pl.pallas_call(
+    near = pl.pallas_call(
         functools.partial(near_kernel, layouts[0], tm),
-        out_shape=jax.ShapeDtypeStruct((time_count * block, columns), jnp.bfloat16),
-        in_specs=[VMEM] * (len(arrays[0]) + tm + 1),
+        out_shape=jax.ShapeDtypeStruct((freq_count, block, columns), jnp.float32),
+        in_specs=[VMEM] * (len(arrays[0]) + tm + 2),
         out_specs=VMEM,
         scratch_shapes=weights,
         compiler_params=large,
         name="near",
-    )(*arrays[0], *scaled, occupation)
+    )(*arrays[0], *scaled, occupation, cosines)
     return pl.pallas_call(
         functools.partial(far_kernel, layouts[1], tm),
         out_shape=result,
@@ -214,7 +217,7 @@
         scratch_shapes=weights + staging,
         compiler_params=large,
         name="far",
-    )(*arrays[1], *scaled, polar, occupation, cosines)
+    )(*arrays[1], *scaled, near, occupation, cosines)
 
 
 def solution(mesh):

time: 27.4 us -> 27.6 us (level)
  transfers between devices with their start and end apart: 12 -> 12, of which waited for: 4 -> 4; matrix products, arithmetic and copies ran while one was open for 6% -> 6% of each run, Pallas kernels for 6% -> 7%
where the time goes in v3:
time: 27.6 us; the launch traced here: 27.4 us
  starting transfers between devices  12.5 us (45%)
  waiting for transfers between devices  9.12 us (33%)
  Pallas kernels  4 us (14%)
  local copies, waits for them, and re-layouts  1.52 us (6%)
    ppermute x12, starting transfers between devices, swap(): return lax.ppermute(value, ('space', 'tm'), pairs)  12.5 us
    ppermute x12, waiting for transfers between devices, swap(): return lax.ppermute(value, ('space', 'tm'), pairs)  9.12 us
    pallas_call x1, Pallas kernels, body(): pl.pallas_call(functools.partial(far_kernel, layouts[1], tm), out_shape=r...  2.21 us
    dynamic_slice x1, local copies, waits for them, and re-layouts, body(): lax.dynamic_slice_in_dim(row_orbitals, (me ^ h) * block, block, 0)  1.27 us
    pallas_call x1, Pallas kernels, body(): pl.pallas_call(functools.partial(near_kernel, layouts[0], tm), out_shape=...  1.06 us
  transfers between devices with their start and end apart: 12, of which 4 were waited for; matrix products, arithmetic and copies ran while one was open for 6% of the time, Pallas kernels for 7%

profile of v3, /device:TPU:0, one launch (start us, length us, event | category | flops | bytes accessed | tf_op | source)
XLA Modules:
  0.0 27.4 jit_solution(16902830794026101835)
XLA Ops:
  0.0 0.0 copy-start.1
  0.0 0.0 copy-start.2
  0.0 0.0 copy-start.3
  0.0 0.0 copy-start.6
  0.0 0.0 copy-start.4
  0.0 0.0 copy-start.5
  0.0 2.5 %collective-permute-start = (bf16[16,1024]{1,0:T(8,128)(2,1)}, bf16[16,1024]{1,0:T(8,128)(2,1)S(1)}, u32[]{:S(2)}, u32[]{:S(2)}) collective-permute-start(bf16[16,1024]{1,0:T(8,128)(2,1)} %param.9), channel_id=1, source_target_pairs={{0,3},{1,2},{2,1},{3,0},{4,7},{5,6},{6,5},{7,4},{8,11},{9,10},{10,... | collective-permute-start | bytes 98312 | tf_op jit(solution)/shard_map/ppermute | solution.py:133
  2.5 1.3 %constant_dynamic-slice_fusion = (bf16[256,1024]{1,0:T(8,128)(2,1)S(1)}, bf16[256,1024]{1,0:T(8,128)(2,1)S(1)}) fusion(bf16[512,1024]{1,0:T(8,128)(2,1)} %param.8, s32[]{:T(128)S(6)} %select_n.21, s32[]{:T(128)S(6)} %select_n.18), kind=kLoop, calls=%fused_computation.16 | loop fusion | bytes 2097160 | tf_op jit(solution)/shard_map/dynamic_slice | solution.py:136
  3.8 0.0 copy-start
  3.8 0.7 %collective-permute-start.7 = (bf16[256,1024]{1,0:T(8,128)(2,1)S(1)}, bf16[256,1024]{1,0:T(8,128)(2,1)S(1)}, u32[]{:S(2)}, u32[]{:S(2)}) collective-permute-start(bf16[256,1024]{1,0:T(8,128)(2,1)S(1)} %get-tuple-element.9), channel_id=1, source_target_pairs={{0,1},{1,0},{2,3},{3,2},{4,5},{5,4},{6,7},{7,6},{8,9},{9,8},{10,11... | collective-permute-start | bytes 1572872 | tf_op jit(solution)/shard_map/ppermute | solution.py:133
  4.4 0.0 copy-done.1
  4.5 0.1 collective-permute-done
  4.6 2.1 %collective-permute-start.8 = (bf16[16,2048]{1,0:T(8,128)(2,1)S(1)}, bf16[16,2048]{1,0:T(8,128)(2,1)S(1)}, u32[]{:S(2)}, u32[]{:S(2)}) collective-permute-start(bf16[16,2048]{1,0:T(8,128)(2,1)S(1)} %constant_dynamic-update-slice_fusion.refs_0_), channel_id=1, source_target_pairs={{0,10},{1,11},{2,8},{3,9},{4,14},{5,15},{6,12},{7,13},{8,2},{9,3},... | collective-permute-start | bytes 196616 | tf_op jit(solution)/shard_map/ppermute | solution.py:133
  6.7 0.0 copy-done.2
  6.8 1.6 %collective-permute-start.9 = (bf16[16,2048]{1,0:T(8,128)(2,1)S(1)}, bf16[16,2048]{1,0:T(8,128)(2,1)S(1)}, u32[]{:S(2)}, u32[]{:S(2)}) collective-permute-start(bf16[16,2048]{1,0:T(8,128)(2,1)S(1)} %constant_dynamic-update-slice_fusion.refs_0_), channel_id=1, source_target_pairs={{0,6},{1,7},{2,4},{3,5},{4,2},{5,3},{6,0},{7,1},{8,14},{9,15},{10,... | collective-permute-start | bytes 196616 | tf_op jit(solution)/shard_map/ppermute | solution.py:133
  8.3 2.3 %collective-permute-start.1 = (bf16[16,2048]{1,0:T(8,128)(2,1)S(1)}, bf16[16,2048]{1,0:T(8,128)(2,1)S(1)}, u32[]{:S(2)}, u32[]{:S(2)}) collective-permute-start(bf16[16,2048]{1,0:T(8,128)(2,1)S(1)} %constant_dynamic-update-slice_fusion.refs_0_), channel_id=1, source_target_pairs={{0,18},{1,19},{2,16},{3,17},{4,22},{5,23},{6,20},{7,21},{8,26},{9,... | collective-permute-start | bytes 196616 | tf_op jit(solution)/shard_map/ppermute | solution.py:133
  10.6 0.0 collective-permute-done.8.refs_1_
  10.6 0.5 %collective-permute-start.10 = (bf16[16,2048]{1,0:T(8,128)(2,1)S(1)}, bf16[16,2048]{1,0:T(8,128)(2,1)S(1)}, u32[]{:S(2)}, u32[]{:S(2)}) collective-permute-start(bf16[16,2048]{1,0:T(8,128)(2,1)S(1)} %collective-permute-done.8.refs_1_), channel_id=1, source_target_pairs={{0,6},{1,7},{2,4},{3,5},{4,2},{5,3},{6,0},{7,1},{8,14},{9,15},{10,... | collective-permute-start | bytes 196616 | tf_op jit(solution)/shard_map/ppermute | solution.py:133
  11.2 0.0 copy-done.3
  11.2 3.7 %collective-permute-done.1.refs_0_ = bf16[16,2048]{1,0:T(8,128)(2,1)S(1)} collective-permute-done((bf16[16,2048]{1,0:T(8,128)(2,1)S(1)}, bf16[16,2048]{1,0:T(8,128)(2,1)S(1)}, u32[]{:S(2)}, u32[]{:S(2)}) %collective-permute-start.1) | collective-permute-done | bytes 65568 | tf_op jit(solution)/shard_map/ppermute | solution.py:133
  14.9 0.1 collective-permute-start.3
  15.0 0.0 collective-permute-start.2
  15.0 0.0 collective-permute-done.9.refs_2_
  15.0 0.0 collective-permute-done.10.refs_3_
  15.0 0.5 %collective-permute-start.11 = (bf16[4,16,2048]{2,1,0:T(8,128)(2,1)S(1)}, bf16[4,16,2048]{2,1,0:T(8,128)(2,1)S(1)}, u32[]{:S(2)}, u32[]{:S(2)}) collective-permute-start(bf16[4,16,2048]{2,1,0:T(8,128)(2,1)S(1)} %pad_maximum_fusion), channel_id=1, source_target_pairs={{0,2},{1,3},{2,0},{3,1},{4,6},{5,7},{6,4},{7,5},{8,10},{9,11},{10,... | collective-permute-start | bytes 786440 | tf_op jit(solution)/shard_map/ppermute | solution.py:133
  15.5 3.3 %collective-permute-done.2.refs_1_ = bf16[16,2048]{1,0:T(8,128)(2,1)S(1)} collective-permute-done((bf16[16,2048]{1,0:T(8,128)(2,1)S(1)}, bf16[16,2048]{1,0:T(8,128)(2,1)S(1)}, u32[]{:S(2)}, u32[]{:S(2)}) %collective-permute-start.2) | collective-permute-done | bytes 65568 | tf_op jit(solution)/shard_map/ppermute | solution.py:133
  18.8 1.7 %collective-permute-start.4 = (bf16[16,2048]{1,0:T(8,128)(2,1)S(1)}, bf16[16,2048]{1,0:T(8,128)(2,1)S(1)}, u32[]{:S(2)}, u32[]{:S(2)}) collective-permute-start(bf16[16,2048]{1,0:T(8,128)(2,1)S(1)} %collective-permute-done.2.refs_1_), channel_id=1, source_target_pairs={{0,6},{1,7},{2,4},{3,5},{4,2},{5,3},{6,0},{7,1},{8,14},{9,15},{10,... | collective-permute-start | bytes 196616 | tf_op jit(solution)/shard_map/ppermute | solution.py:133
  20.5 0.0 collective-permute-done.3.refs_2_
  20.5 0.2 collective-permute-start.5
  20.7 1.9 %collective-permute-done.4.refs_3_ = bf16[16,2048]{1,0:T(8,128)(2,1)S(1)} collective-permute-done((bf16[16,2048]{1,0:T(8,128)(2,1)S(1)}, bf16[16,2048]{1,0:T(8,128)(2,1)S(1)}, u32[]{:S(2)}, u32[]{:S(2)}) %collective-permute-start.4) | collective-permute-done | bytes 65568 | tf_op jit(solution)/shard_map/ppermute | solution.py:133
  22.6 0.4 %collective-permute-start.6 = (bf16[16,2048]{1,0:T(8,128)(2,1)S(1)}, bf16[16,2048]{1,0:T(8,128)(2,1)S(1)}, u32[]{:S(2)}, u32[]{:S(2)}) collective-permute-start(bf16[16,2048]{1,0:T(8,128)(2,1)S(1)} %collective-permute-done.4.refs_3_), channel_id=1, source_target_pairs={{0,2},{1,3},{2,0},{3,1},{4,6},{5,7},{6,4},{7,5},{8,10},{9,11},{10,... | collective-permute-start | bytes 196616 | tf_op jit(solution)/shard_map/ppermute | solution.py:133
  23.0 0.0 copy-done.6
  23.0 0.0 copy-done.4
  23.0 0.0 copy-done.5
  23.0 0.1 cosine_multiply_fusion
  23.1 0.1 mul.46
  23.2 0.1 broadcast_in_dim.4.times_ref
  23.3 0.4 %own.1 = (bf16[512,1024]{1,0:T(8,128)(2,1)S(1)}, f32[2,16,128]{2,1,0:T(8,128)S(1)}) custom-call(bf16[256,1024]{1,0:T(8,128)(2,1)S(1)} %get-tuple-element.10.rows_ref, f32[16,128]{1,0:T(8,128)S(1)} %negate_bitcast_fusion.levels_ref, s32[16,128]{1,0:T(8,128)S(1)} %get-tuple-element.12.page_ref, s32[16,128]{1,0:T(8,128)S(1)} %get-tuple-element.11.lane_ref, ...), custom_call_target="tpu_custom_call" | custom-call | tf_op jit(solution)/shard_map/own/pallas_call | solution.py:157
  23.7 0.0 collective-permute-done.7.rows_ref
  23.7 0.3 %shard_map.82.refs_6_.refs_7_ = bf16[512,1024]{1,0:T(8,128)(2,1)S(1)} custom-call(bf16[256,1024]{1,0:T(8,128)(2,1)S(1)} %collective-permute-done.7.rows_ref, f32[2,16,128]{2,1,0:T(8,128)S(1)} %get-tuple-element.8.decay_ref), custom_call_target="tpu_custom_call" | custom-call | tf_op jit(solution)/shard_map/pallas_call | solution.py:178
  24.0 0.0 collective-permute-done.11.refs_4_
  24.0 0.1 broadcast_in_dim.5.refs_8_.refs_10_
  24.1 0.0 copy-done
  24.1 1.1 %near.1.refs_8_ = f32[8,256,128]{2,1,0:T(8,128)S(1)} custom-call(bf16[16,2048]{1,0:T(8,128)(2,1)S(1)} %constant_dynamic-update-slice_fusion.refs_0_, bf16[16,2048]{1,0:T(8,128)(2,1)S(1)} %collective-permute-done.8.refs_1_, bf16[16,2048]{1,0:T(8,128)(2,1)S(1)} %collective-permute-done.9.refs_2_, bf16[16,2048]{1,0:T(8,128)(2,1)S(1)} %collective-permute-done.10.refs_3_, ...), custom_call_target="tpu_custom_call" | custom-call | tf_op jit(solution)/shard_map/near/pallas_call | solution.py:203
  25.2 0.0 collective-permute-done.6.refs_5_
  25.2 0.0 collective-permute-done.5.refs_4_
  25.2 2.2 %far.1 = f32[8,256,256]{2,1,0:T(8,128)} custom-call(bf16[16,2048]{1,0:T(8,128)(2,1)S(1)} %collective-permute-done.1.refs_0_, bf16[16,2048]{1,0:T(8,128)(2,1)S(1)} %collective-permute-done.2.refs_1_, bf16[16,2048]{1,0:T(8,128)(2,1)S(1)} %collective-permute-done.3.refs_2_, bf16[16,2048]{1,0:T(8,128)(2,1)S(1)} %collective-permute-done.4.refs_3_, ...), custom_call_target="tpu_custom_call" | custom-call | tf_op jit(solution)/shard_map/far/pallas_call | solution.py:212
  (6 shorter events, 0.1 us)
Async XLA Ops:
  0.0 4.5 %copy-start.1 = (bf16[16,1024]{1,0:T(8,128)(2,1)S(1)}, bf16[16,1024]{1,0:T(8,128)(2,1)}, u32[]{:S(2)}) copy-start(bf16[16,1024]{1,0:T(8,128)(2,1)} %param.9) | copy-start | bytes 98308
  0.0 6.7 %copy-start.2 = (s32[2048]{0:T(1024)S(1)}, s32[2048]{0:T(1024)}, u32[]{:S(2)}) copy-start(s32[2048]{0:T(1024)} %param.11) | copy-start | bytes 24580
  0.0 11.2 %copy-start.3 = (f32[2048]{0:T(1024)S(1)}, f32[2048]{0:T(1024)}, u32[]{:S(2)}) copy-start(f32[2048]{0:T(1024)} %param.12) | copy-start | bytes 24580
  0.0 23.0 %copy-start.6 = (f32[2]{0:T(128)S(1)}, f32[2]{0:T(128)}, u32[]{:S(2)}) copy-start(f32[2]{0:T(128)} %param.13) | copy-start | bytes 28
  0.0 23.0 %copy-start.4 = (f32[8]{0:T(128)S(1)}, f32[8]{0:T(128)}, u32[]{:S(2)}) copy-start(f32[8]{0:T(128)} %param.15) | copy-start | bytes 100
  0.0 23.0 %copy-start.5 = (f32[2]{0:T(128)S(1)}, f32[2]{0:T(128)}, u32[]{:S(2)}) copy-start(f32[2]{0:T(128)} %param.14) | copy-start | bytes 28
  0.0 4.6 %collective-permute-start = (bf16[16,1024]{1,0:T(8,128)(2,1)}, bf16[16,1024]{1,0:T(8,128)(2,1)S(1)}, u32[]{:S(2)}, u32[]{:S(2)}) collective-permute-start(bf16[16,1024]{1,0:T(8,128)(2,1)} %param.9), channel_id=1, source_target_pairs={{0,3},{1,2},{2,1},{3,0},{4,7},{5,6},{6,5},{7,4},{8,11},{9,10},{10,... | collective-permute-start | bytes 98312 | tf_op jit(solution)/shard_map/ppermute | solution.py:133
  3.8 20.3 %copy-start = (s32[2048]{0:T(1024)S(1)}, s32[2048]{0:T(1024)}, u32[]{:S(2)}) copy-start(s32[2048]{0:T(1024)} %param.10) | copy-start | bytes 24580
  3.8 19.9 %collective-permute-start.7 = (bf16[256,1024]{1,0:T(8,128)(2,1)S(1)}, bf16[256,1024]{1,0:T(8,128)(2,1)S(1)}, u32[]{:S(2)}, u32[]{:S(2)}) collective-permute-start(bf16[256,1024]{1,0:T(8,128)(2,1)S(1)} %get-tuple-element.9), channel_id=1, source_target_pairs={{0,1},{1,0},{2,3},{3,2},{4,5},{5,4},{6,7},{7,6},{8,9},{9,8},{10,11... | collective-permute-start | bytes 1572872 | tf_op jit(solution)/shard_map/ppermute | solution.py:133
  4.6 6.0 %collective-permute-start.8 = (bf16[16,2048]{1,0:T(8,128)(2,1)S(1)}, bf16[16,2048]{1,0:T(8,128)(2,1)S(1)}, u32[]{:S(2)}, u32[]{:S(2)}) collective-permute-start(bf16[16,2048]{1,0:T(8,128)(2,1)S(1)} %constant_dynamic-update-slice_fusion.refs_0_), channel_id=1, source_target_pairs={{0,10},{1,11},{2,8},{3,9},{4,14},{5,15},{6,12},{7,13},{8,2},{9,3},... | collective-permute-start | bytes 196616 | tf_op jit(solution)/shard_map/ppermute | solution.py:133
  6.8 8.2 %collective-permute-start.9 = (bf16[16,2048]{1,0:T(8,128)(2,1)S(1)}, bf16[16,2048]{1,0:T(8,128)(2,1)S(1)}, u32[]{:S(2)}, u32[]{:S(2)}) collective-permute-start(bf16[16,2048]{1,0:T(8,128)(2,1)S(1)} %constant_dynamic-update-slice_fusion.refs_0_), channel_id=1, source_target_pairs={{0,6},{1,7},{2,4},{3,5},{4,2},{5,3},{6,0},{7,1},{8,14},{9,15},{10,... | collective-permute-start | bytes 196616 | tf_op jit(solution)/shard_map/ppermute | solution.py:133
  8.3 6.6 %collective-permute-start.1 = (bf16[16,2048]{1,0:T(8,128)(2,1)S(1)}, bf16[16,2048]{1,0:T(8,128)(2,1)S(1)}, u32[]{:S(2)}, u32[]{:S(2)}) collective-permute-start(bf16[16,2048]{1,0:T(8,128)(2,1)S(1)} %constant_dynamic-update-slice_fusion.refs_0_), channel_id=1, source_target_pairs={{0,18},{1,19},{2,16},{3,17},{4,22},{5,23},{6,20},{7,21},{8,26},{9,... | collective-permute-start | bytes 196616 | tf_op jit(solution)/shard_map/ppermute | solution.py:133
  10.6 4.3 %collective-permute-start.10 = (bf16[16,2048]{1,0:T(8,128)(2,1)S(1)}, bf16[16,2048]{1,0:T(8,128)(2,1)S(1)}, u32[]{:S(2)}, u32[]{:S(2)}) collective-permute-start(bf16[16,2048]{1,0:T(8,128)(2,1)S(1)} %collective-permute-done.8.refs_1_), channel_id=1, source_target_pairs={{0,6},{1,7},{2,4},{3,5},{4,2},{5,3},{6,0},{7,1},{8,14},{9,15},{10,... | collective-permute-start | bytes 196616 | tf_op jit(solution)/shard_map/ppermute | solution.py:133
  14.9 5.6 %collective-permute-start.3 = (bf16[16,2048]{1,0:T(8,128)(2,1)S(1)}, bf16[16,2048]{1,0:T(8,128)(2,1)S(1)}, u32[]{:S(2)}, u32[]{:S(2)}) collective-permute-start(bf16[16,2048]{1,0:T(8,128)(2,1)S(1)} %collective-permute-done.1.refs_0_), channel_id=1, source_target_pairs={{0,6},{1,7},{2,4},{3,5},{4,2},{5,3},{6,0},{7,1},{8,14},{9,15},{10,... | collective-permute-start | bytes 196616 | tf_op jit(solution)/shard_map/ppermute | solution.py:133
  15.0 3.8 %collective-permute-start.2 = (bf16[16,2048]{1,0:T(8,128)(2,1)S(1)}, bf16[16,2048]{1,0:T(8,128)(2,1)S(1)}, u32[]{:S(2)}, u32[]{:S(2)}) collective-permute-start(bf16[16,2048]{1,0:T(8,128)(2,1)S(1)} %collective-permute-done.1.refs_0_), channel_id=1, source_target_pairs={{0,10},{1,11},{2,8},{3,9},{4,14},{5,15},{6,12},{7,13},{8,2},{9,3},... | collective-permute-start | bytes 196616 | tf_op jit(solution)/shard_map/ppermute | solution.py:133
  15.0 9.0 %collective-permute-start.11 = (bf16[4,16,2048]{2,1,0:T(8,128)(2,1)S(1)}, bf16[4,16,2048]{2,1,0:T(8,128)(2,1)S(1)}, u32[]{:S(2)}, u32[]{:S(2)}) collective-permute-start(bf16[4,16,2048]{2,1,0:T(8,128)(2,1)S(1)} %pad_maximum_fusion), channel_id=1, source_target_pairs={{0,2},{1,3},{2,0},{3,1},{4,6},{5,7},{6,4},{7,5},{8,10},{9,11},{10,... | collective-permute-start | bytes 786440 | tf_op jit(solution)/shard_map/ppermute | solution.py:133
  18.8 3.8 %collective-permute-start.4 = (bf16[16,2048]{1,0:T(8,128)(2,1)S(1)}, bf16[16,2048]{1,0:T(8,128)(2,1)S(1)}, u32[]{:S(2)}, u32[]{:S(2)}) collective-permute-start(bf16[16,2048]{1,0:T(8,128)(2,1)S(1)} %collective-permute-done.2.refs_1_), channel_id=1, source_target_pairs={{0,6},{1,7},{2,4},{3,5},{4,2},{5,3},{6,0},{7,1},{8,14},{9,15},{10,... | collective-permute-start | bytes 196616 | tf_op jit(solution)/shard_map/ppermute | solution.py:133
  20.5 4.7 %collective-permute-start.5 = (bf16[3,16,2048]{2,1,0:T(8,128)(2,1)S(1)}, bf16[3,16,2048]{2,1,0:T(8,128)(2,1)S(1)}, u32[]{:S(2)}, u32[]{:S(2)}) collective-permute-start(bf16[3,16,2048]{2,1,0:T(8,128)(2,1)S(1)} %pad_maximum_fusion.1), channel_id=1, source_target_pairs={{0,2},{1,3},{2,0},{3,1},{4,6},{5,7},{6,4},{7,5},{8,10},{9,11},{10,... | collective-permute-start | bytes 589832 | tf_op jit(solution)/shard_map/ppermute | solution.py:133
  22.6 2.6 %collective-permute-start.6 = (bf16[16,2048]{1,0:T(8,128)(2,1)S(1)}, bf16[16,2048]{1,0:T(8,128)(2,1)S(1)}, u32[]{:S(2)}, u32[]{:S(2)}) collective-permute-start(bf16[16,2048]{1,0:T(8,128)(2,1)S(1)} %collective-permute-done.4.refs_3_), channel_id=1, source_target_pairs={{0,2},{1,3},{2,0},{3,1},{4,6},{5,7},{6,4},{7,5},{8,10},{9,11},{10,... | collective-permute-start | bytes 196616 | tf_op jit(solution)/shard_map/ppermute | solution.py:133

commit v4 on v3

--- a/solution.py
+++ b/solution.py
@@ -154,6 +154,7 @@
     pages = (-1, LANES)
     small = pltpu.CompilerParams(vmem_limit_bytes=8 * MIB)
     table = (levels.shape[0] // LANES, LANES)
+    tables = -levels.reshape(pages), (order // LANES).reshape(pages), (order % LANES).reshape(pages)
     own_scaled, decays = pl.pallas_call(
         own_kernel,
         out_shape=(
@@ -165,10 +166,8 @@
         compiler_params=small,
         name="own",
     )(
-        lax.dynamic_slice_in_dim(row_orbitals, me * block, block, 0),
-        -levels.reshape(pages),
-        (order // LANES).reshape(pages),
-        (order % LANES).reshape(pages),
+        lax.dynamic_slice_in_dim(lax.optimization_barrier((row_orbitals, unit))[0], me * block, block, 0),
+        *tables,
         jnp.broadcast_to(times[:, None], (time_count, LANES)),
     )
 

time: 27.6 us -> 29.2 us (1.058)
  waiting for transfers between devices: 9.12 us -> 6.39 us
  starting transfers between devices: 12.5 us -> 15.2 us
  other arithmetic: 0.18 us -> 2.25 us
  local copies, waits for them, and re-layouts: 1.52 us -> 1.08 us
    ppermute x12, waiting for transfers between devices: 9.12 us -> 6.39 us  [swap(): return lax.ppermute(value, ('space', 'tm'), pairs)]
    ppermute x12, starting transfers between devices: 12.5 us -> 15.2 us  [swap(): return lax.ppermute(value, ('space', 'tm'), pairs)]
    dynamic_slice x1, local copies, waits for them, and re-layouts: 1.27 us -> 0.03 us  [body(): lax.dynamic_slice_in_dim(row_orbitals, (me ^ h) * block, block, 0)]
    unnamed x15 -> x11, local copies, waits for them, and re-layouts: 0.03 us -> 0.78 us
    neg x1, other arithmetic: 0.01 us -> 0.7 us  [body(): -levels.reshape(pages)]
    reshape x1, other arithmetic: 0.01 us -> 0.71 us  [body(): (order % LANES).reshape(pages)]
    another operation x2, other arithmetic: 0.06 us -> 0.74 us  [body(): jnp.stack([held[o] for o in group])]
  transfers between devices with their start and end apart: 12 -> 12, of which waited for: 4 -> 4; matrix products, arithmetic and copies ran while one was open for 6% -> 11% of each run, Pallas kernels for 7% -> 6%
where the time goes in v4:
time: 29.2 us; the launch traced here: 29 us
  starting transfers between devices  15.2 us (52%)
  waiting for transfers between devices  6.39 us (22%)
  Pallas kernels  3.99 us (14%)
  other arithmetic  2.25 us (8%)
  local copies, waits for them, and re-layouts  1.08 us (4%)
    ppermute x12, starting transfers between devices, swap(): return lax.ppermute(value, ('space', 'tm'), pairs)  15.2 us
    ppermute x12, waiting for transfers between devices, swap(): return lax.ppermute(value, ('space', 'tm'), pairs)  6.39 us
    pallas_call x1, Pallas kernels, body(): pl.pallas_call(functools.partial(far_kernel, layouts[1], tm), out_shape=r...  2.2 us
    pallas_call x1, Pallas kernels, body(): pl.pallas_call(functools.partial(near_kernel, layouts[0], tm), out_shape=...  1.06 us
    unnamed x11, local copies, waits for them, and re-layouts  0.78 us
    another operation x2, other arithmetic, body(): jnp.stack([held[o] for o in group])  0.74 us
    reshape x1, other arithmetic, body(): (order % LANES).reshape(pages)  0.71 us
    neg x1, other arithmetic, body(): -levels.reshape(pages)  0.7 us
  transfers between devices with their start and end apart: 12, of which 4 were waited for; matrix products, arithmetic and copies ran while one was open for 11% of the time, Pallas kernels for 6%

profile of v4, /device:TPU:0, one launch (start us, length us, event | category | flops | bytes accessed | tf_op | source)
XLA Modules:
  0.0 29.0 jit_solution(17609979762474663781)
XLA Ops:
  0.0 0.0 copy-start
  0.0 0.0 copy-start.4
  0.0 0.0 copy-start.2
  0.0 0.0 copy-start.3
  0.0 2.5 %collective-permute-start = (bf16[16,1024]{1,0:T(8,128)(2,1)}, bf16[16,1024]{1,0:T(8,128)(2,1)S(1)}, u32[]{:S(2)}, u32[]{:S(2)}) collective-permute-start(bf16[16,1024]{1,0:T(8,128)(2,1)} %param.9), channel_id=1, source_target_pairs={{0,3},{1,2},{2,1},{3,0},{4,7},{5,6},{6,5},{7,4},{8,11},{9,10},{10,... | collective-permute-start | bytes 98312 | tf_op jit(solution)/shard_map/ppermute | solution.py:133
  2.5 0.0 copy-done
  2.5 1.8 %collective-permute-start.7 = (bf16[256,1024]{1,0:T(8,128)(2,1)S(1)}, bf16[256,1024]{1,0:T(8,128)(2,1)S(1)}, u32[]{:S(2)}, u32[]{:S(2)}) collective-permute-start(bf16[256,1024]{1,0:T(8,128)(2,1)S(1)} %constant_dynamic-slice_fusion), channel_id=1, source_target_pairs={{0,1},{1,0},{2,3},{3,2},{4,5},{5,4},{6,7},{7,6},{8,9},{9,8},{10,11... | collective-permute-start | bytes 1572872 | tf_op jit(solution)/shard_map/ppermute | solution.py:133
  4.3 0.8 %constant_dynamic-update-slice_fusion.1 = bf16[16,2048]{1,0:T(8,128)(2,1)S(1)} fusion(bf16[16,1024]{1,0:T(8,128)(2,1)} %param.9), kind=kLoop, calls=%fused_computation.13 | loop fusion | bytes 65536
  5.1 0.0 collective-permute-done
  5.1 0.0 copy-start.1
  5.1 2.6 %collective-permute-start.1 = (bf16[16,2048]{1,0:T(8,128)(2,1)S(1)}, bf16[16,2048]{1,0:T(8,128)(2,1)S(1)}, u32[]{:S(2)}, u32[]{:S(2)}) collective-permute-start(bf16[16,2048]{1,0:T(8,128)(2,1)S(1)} %constant_dynamic-update-slice_fusion.refs_0_), channel_id=1, source_target_pairs={{0,18},{1,19},{2,16},{3,17},{4,22},{5,23},{6,20},{7,21},{8,26},{9,... | collective-permute-start | bytes 196616 | tf_op jit(solution)/shard_map/ppermute | solution.py:133
  7.7 0.7 %fusion.1 = (s32[16,128]{1,0:T(8,128)S(1)}, s32[16,128]{1,0:T(8,128)S(1)}) fusion(s32[2048]{0:T(1024)} %param.11), kind=kLoop, calls=%fused_computation.8 | loop fusion | flops 38912 | bytes 24576 | tf_op jit(solution)/shard_map/reshape | solution.py:157
  8.4 1.6 %collective-permute-start.8 = (bf16[16,2048]{1,0:T(8,128)(2,1)S(1)}, bf16[16,2048]{1,0:T(8,128)(2,1)S(1)}, u32[]{:S(2)}, u32[]{:S(2)}) collective-permute-start(bf16[16,2048]{1,0:T(8,128)(2,1)S(1)} %constant_dynamic-update-slice_fusion.refs_0_), channel_id=1, source_target_pairs={{0,10},{1,11},{2,8},{3,9},{4,14},{5,15},{6,12},{7,13},{8,2},{9,3},... | collective-permute-start | bytes 196616 | tf_op jit(solution)/shard_map/ppermute | solution.py:133
  10.1 0.0 collective-permute-done.1.refs_0_
  10.1 3.1 %collective-permute-start.3 = (bf16[16,2048]{1,0:T(8,128)(2,1)S(1)}, bf16[16,2048]{1,0:T(8,128)(2,1)S(1)}, u32[]{:S(2)}, u32[]{:S(2)}) collective-permute-start(bf16[16,2048]{1,0:T(8,128)(2,1)S(1)} %collective-permute-done.1.refs_0_), channel_id=1, source_target_pairs={{0,6},{1,7},{2,4},{3,5},{4,2},{5,3},{6,0},{7,1},{8,14},{9,15},{10,... | collective-permute-start | bytes 196616 | tf_op jit(solution)/shard_map/ppermute | solution.py:133
  13.2 0.9 %collective-permute-start.2 = (bf16[16,2048]{1,0:T(8,128)(2,1)S(1)}, bf16[16,2048]{1,0:T(8,128)(2,1)S(1)}, u32[]{:S(2)}, u32[]{:S(2)}) collective-permute-start(bf16[16,2048]{1,0:T(8,128)(2,1)S(1)} %collective-permute-done.1.refs_0_), channel_id=1, source_target_pairs={{0,10},{1,11},{2,8},{3,9},{4,14},{5,15},{6,12},{7,13},{8,2},{9,3},... | collective-permute-start | bytes 196616 | tf_op jit(solution)/shard_map/ppermute | solution.py:133
  14.1 0.7 %negate_bitcast_fusion.levels_ref = f32[16,128]{1,0:T(8,128)S(1)} fusion(f32[2048]{0:T(1024)} %param.12), kind=kLoop, calls=%fused_computation.10 | loop fusion | flops 2048 | bytes 16384 | tf_op jit(solution)/shard_map/neg | solution.py:157
  14.8 0.2 collective-permute-start.9
  14.9 0.0 collective-permute-done.8.refs_1_
  14.9 1.6 %collective-permute-start.10 = (bf16[16,2048]{1,0:T(8,128)(2,1)S(1)}, bf16[16,2048]{1,0:T(8,128)(2,1)S(1)}, u32[]{:S(2)}, u32[]{:S(2)}) collective-permute-start(bf16[16,2048]{1,0:T(8,128)(2,1)S(1)} %collective-permute-done.8.refs_1_), channel_id=1, source_target_pairs={{0,6},{1,7},{2,4},{3,5},{4,2},{5,3},{6,0},{7,1},{8,14},{9,15},{10,... | collective-permute-start | bytes 196616 | tf_op jit(solution)/shard_map/ppermute | solution.py:133
  16.5 0.0 collective-permute-done.3.refs_2_
  16.5 0.4 %collective-permute-done.2.refs_1_ = bf16[16,2048]{1,0:T(8,128)(2,1)S(1)} collective-permute-done((bf16[16,2048]{1,0:T(8,128)(2,1)S(1)}, bf16[16,2048]{1,0:T(8,128)(2,1)S(1)}, u32[]{:S(2)}, u32[]{:S(2)}) %collective-permute-start.2) | collective-permute-done | bytes 65568 | tf_op jit(solution)/shard_map/ppermute | solution.py:133
  16.9 0.7 %pad_maximum_fusion.1 = bf16[3,16,2048]{2,1,0:T(8,128)(2,1)} fusion(bf16[1,16,2048]{2,1,0:T(8,128)(2,1)S(1)} %bitcast.16, bf16[1,16,2048]{2,1,0:T(8,128)(2,1)S(1)} %bitcast.17, bf16[1,16,2048]{2,1,0:T(8,128)(2,1)S(1)} %bitcast.15), kind=kLoop, calls=%fused_computation.1 | loop fusion | flops 196608 | bytes 393216 | tf_op jit(solution)/shard_map/stack | solution.py:151
  17.6 0.0 collective-permute-start.5
  17.7 1.2 %collective-permute-done.9.refs_2_ = bf16[16,2048]{1,0:T(8,128)(2,1)S(1)} collective-permute-done((bf16[16,2048]{1,0:T(8,128)(2,1)S(1)}, bf16[16,2048]{1,0:T(8,128)(2,1)S(1)}, u32[]{:S(2)}, u32[]{:S(2)}) %collective-permute-start.9) | collective-permute-done | bytes 65568 | tf_op jit(solution)/shard_map/ppermute | solution.py:133
  18.9 1.4 %collective-permute-done.10.refs_3_ = bf16[16,2048]{1,0:T(8,128)(2,1)S(1)} collective-permute-done((bf16[16,2048]{1,0:T(8,128)(2,1)S(1)}, bf16[16,2048]{1,0:T(8,128)(2,1)S(1)}, u32[]{:S(2)}, u32[]{:S(2)}) %collective-permute-start.10) | collective-permute-done | bytes 65568 | tf_op jit(solution)/shard_map/ppermute | solution.py:133
  20.3 0.2 collective-permute-start.11
  20.5 0.3 %collective-permute-start.4 = (bf16[16,2048]{1,0:T(8,128)(2,1)S(1)}, bf16[16,2048]{1,0:T(8,128)(2,1)S(1)}, u32[]{:S(2)}, u32[]{:S(2)}) collective-permute-start(bf16[16,2048]{1,0:T(8,128)(2,1)S(1)} %collective-permute-done.2.refs_1_), channel_id=1, source_target_pairs={{0,6},{1,7},{2,4},{3,5},{4,2},{5,3},{6,0},{7,1},{8,14},{9,15},{10,... | collective-permute-start | bytes 196616 | tf_op jit(solution)/shard_map/ppermute | solution.py:133
  20.9 0.0 copy-done.4
  20.9 0.0 copy-done.2
  20.9 0.0 copy-done.3
  20.9 0.1 cosine_multiply_fusion
  21.0 0.1 mul.46
  21.1 3.3 %collective-permute-done.4.refs_3_ = bf16[16,2048]{1,0:T(8,128)(2,1)S(1)} collective-permute-done((bf16[16,2048]{1,0:T(8,128)(2,1)S(1)}, bf16[16,2048]{1,0:T(8,128)(2,1)S(1)}, u32[]{:S(2)}, u32[]{:S(2)}) %collective-permute-start.4) | collective-permute-done | bytes 65568 | tf_op jit(solution)/shard_map/ppermute | solution.py:133
  24.3 0.4 %collective-permute-start.6 = (bf16[16,2048]{1,0:T(8,128)(2,1)S(1)}, bf16[16,2048]{1,0:T(8,128)(2,1)S(1)}, u32[]{:S(2)}, u32[]{:S(2)}) collective-permute-start(bf16[16,2048]{1,0:T(8,128)(2,1)S(1)} %collective-permute-done.4.refs_3_), channel_id=1, source_target_pairs={{0,2},{1,3},{2,0},{3,1},{4,6},{5,7},{6,4},{7,5},{8,10},{9,11},{10,... | collective-permute-start | bytes 196616 | tf_op jit(solution)/shard_map/ppermute | solution.py:133
  24.8 0.1 broadcast_in_dim.4.times_ref
  24.8 0.4 %own.1 = (bf16[512,1024]{1,0:T(8,128)(2,1)S(1)}, f32[2,16,128]{2,1,0:T(8,128)S(1)}) custom-call(bf16[256,1024]{1,0:T(8,128)(2,1)S(1)} %constant_dynamic-slice_fusion.1.rows_ref, f32[16,128]{1,0:T(8,128)S(1)} %negate_bitcast_fusion.levels_ref, s32[16,128]{1,0:T(8,128)S(1)} %get-tuple-element.12.page_ref, s32[16,128]{1,0:T(8,128)S(1)} %get-tuple-element.11.lane_ref, ...), custom_call_target="tpu_custom_call" | custom-call | tf_op jit(solution)/shard_map/own/pallas_call | solution.py:158
  25.3 0.0 collective-permute-done.7.rows_ref
  25.3 0.3 %shard_map.82.refs_6_.refs_7_ = bf16[512,1024]{1,0:T(8,128)(2,1)S(1)} custom-call(bf16[256,1024]{1,0:T(8,128)(2,1)S(1)} %collective-permute-done.7.rows_ref, f32[2,16,128]{2,1,0:T(8,128)S(1)} %get-tuple-element.10.decay_ref), custom_call_target="tpu_custom_call" | custom-call | tf_op jit(solution)/shard_map/pallas_call | solution.py:177
  25.6 0.0 collective-permute-done.11.refs_4_
  25.6 0.1 broadcast_in_dim.5.refs_8_.refs_10_
  25.7 0.0 copy-done.1
  25.7 1.1 %near.1.refs_8_ = f32[8,256,128]{2,1,0:T(8,128)S(1)} custom-call(bf16[16,2048]{1,0:T(8,128)(2,1)S(1)} %constant_dynamic-update-slice_fusion.refs_0_, bf16[16,2048]{1,0:T(8,128)(2,1)S(1)} %collective-permute-done.8.refs_1_, bf16[16,2048]{1,0:T(8,128)(2,1)S(1)} %collective-permute-done.9.refs_2_, bf16[16,2048]{1,0:T(8,128)(2,1)S(1)} %collective-permute-done.10.refs_3_, ...), custom_call_target="tpu_custom_call" | custom-call | tf_op jit(solution)/shard_map/near/pallas_call | solution.py:202
  26.7 0.0 collective-permute-done.6.refs_5_
  26.8 0.0 collective-permute-done.5.refs_4_
  26.8 2.2 %far.1 = f32[8,256,256]{2,1,0:T(8,128)} custom-call(bf16[16,2048]{1,0:T(8,128)(2,1)S(1)} %collective-permute-done.1.refs_0_, bf16[16,2048]{1,0:T(8,128)(2,1)S(1)} %collective-permute-done.2.refs_1_, bf16[16,2048]{1,0:T(8,128)(2,1)S(1)} %collective-permute-done.3.refs_2_, bf16[16,2048]{1,0:T(8,128)(2,1)S(1)} %collective-permute-done.4.refs_3_, ...), custom_call_target="tpu_custom_call" | custom-call | tf_op jit(solution)/shard_map/far/pallas_call | solution.py:211
  (4 shorter events, 0.1 us)
Async XLA Ops:
  0.0 2.5 %copy-start = (bf16[512,1024]{1,0:T(8,128)(2,1)S(1)}, bf16[512,1024]{1,0:T(8,128)(2,1)}, u32[]{:S(2)}) copy-start(bf16[512,1024]{1,0:T(8,128)(2,1)} %param.8) | copy-start | bytes 3145732
  0.0 20.9 %copy-start.4 = (f32[2]{0:T(128)S(1)}, f32[2]{0:T(128)}, u32[]{:S(2)}) copy-start(f32[2]{0:T(128)} %param.13) | copy-start | bytes 28
  0.0 20.9 %copy-start.2 = (f32[8]{0:T(128)S(1)}, f32[8]{0:T(128)}, u32[]{:S(2)}) copy-start(f32[8]{0:T(128)} %param.15) | copy-start | bytes 100
  0.0 20.9 %copy-start.3 = (f32[2]{0:T(128)S(1)}, f32[2]{0:T(128)}, u32[]{:S(2)}) copy-start(f32[2]{0:T(128)} %param.14) | copy-start | bytes 28
  0.0 5.0 %collective-permute-start = (bf16[16,1024]{1,0:T(8,128)(2,1)}, bf16[16,1024]{1,0:T(8,128)(2,1)S(1)}, u32[]{:S(2)}, u32[]{:S(2)}) collective-permute-start(bf16[16,1024]{1,0:T(8,128)(2,1)} %param.9), channel_id=1, source_target_pairs={{0,3},{1,2},{2,1},{3,0},{4,7},{5,6},{6,5},{7,4},{8,11},{9,10},{10,... | collective-permute-start | bytes 98312 | tf_op jit(solution)/shard_map/ppermute | solution.py:133
  2.5 22.8 %collective-permute-start.7 = (bf16[256,1024]{1,0:T(8,128)(2,1)S(1)}, bf16[256,1024]{1,0:T(8,128)(2,1)S(1)}, u32[]{:S(2)}, u32[]{:S(2)}) collective-permute-start(bf16[256,1024]{1,0:T(8,128)(2,1)S(1)} %constant_dynamic-slice_fusion), channel_id=1, source_target_pairs={{0,1},{1,0},{2,3},{3,2},{4,5},{5,4},{6,7},{7,6},{8,9},{9,8},{10,11... | collective-permute-start | bytes 1572872 | tf_op jit(solution)/shard_map/ppermute | solution.py:133
  5.1 20.6 %copy-start.1 = (s32[2048]{0:T(1024)S(1)}, s32[2048]{0:T(1024)}, u32[]{:S(2)}) copy-start(s32[2048]{0:T(1024)} %param.10) | copy-start | bytes 24580
  5.1 5.0 %collective-permute-start.1 = (bf16[16,2048]{1,0:T(8,128)(2,1)S(1)}, bf16[16,2048]{1,0:T(8,128)(2,1)S(1)}, u32[]{:S(2)}, u32[]{:S(2)}) collective-permute-start(bf16[16,2048]{1,0:T(8,128)(2,1)S(1)} %constant_dynamic-update-slice_fusion.refs_0_), channel_id=1, source_target_pairs={{0,18},{1,19},{2,16},{3,17},{4,22},{5,23},{6,20},{7,21},{8,26},{9,... | collective-permute-start | bytes 196616 | tf_op jit(solution)/shard_map/ppermute | solution.py:133
  8.4 6.5 %collective-permute-start.8 = (bf16[16,2048]{1,0:T(8,128)(2,1)S(1)}, bf16[16,2048]{1,0:T(8,128)(2,1)S(1)}, u32[]{:S(2)}, u32[]{:S(2)}) collective-permute-start(bf16[16,2048]{1,0:T(8,128)(2,1)S(1)} %constant_dynamic-update-slice_fusion.refs_0_), channel_id=1, source_target_pairs={{0,10},{1,11},{2,8},{3,9},{4,14},{5,15},{6,12},{7,13},{8,2},{9,3},... | collective-permute-start | bytes 196616 | tf_op jit(solution)/shard_map/ppermute | solution.py:133
  10.1 6.4 %collective-permute-start.3 = (bf16[16,2048]{1,0:T(8,128)(2,1)S(1)}, bf16[16,2048]{1,0:T(8,128)(2,1)S(1)}, u32[]{:S(2)}, u32[]{:S(2)}) collective-permute-start(bf16[16,2048]{1,0:T(8,128)(2,1)S(1)} %collective-permute-done.1.refs_0_), channel_id=1, source_target_pairs={{0,6},{1,7},{2,4},{3,5},{4,2},{5,3},{6,0},{7,1},{8,14},{9,15},{10,... | collective-permute-start | bytes 196616 | tf_op jit(solution)/shard_map/ppermute | solution.py:133
  13.2 3.8 %collective-permute-start.2 = (bf16[16,2048]{1,0:T(8,128)(2,1)S(1)}, bf16[16,2048]{1,0:T(8,128)(2,1)S(1)}, u32[]{:S(2)}, u32[]{:S(2)}) collective-permute-start(bf16[16,2048]{1,0:T(8,128)(2,1)S(1)} %collective-permute-done.1.refs_0_), channel_id=1, source_target_pairs={{0,10},{1,11},{2,8},{3,9},{4,14},{5,15},{6,12},{7,13},{8,2},{9,3},... | collective-permute-start | bytes 196616 | tf_op jit(solution)/shard_map/ppermute | solution.py:133
  14.8 4.1 %collective-permute-start.9 = (bf16[16,2048]{1,0:T(8,128)(2,1)S(1)}, bf16[16,2048]{1,0:T(8,128)(2,1)S(1)}, u32[]{:S(2)}, u32[]{:S(2)}) collective-permute-start(bf16[16,2048]{1,0:T(8,128)(2,1)S(1)} %constant_dynamic-update-slice_fusion.refs_0_), channel_id=1, source_target_pairs={{0,6},{1,7},{2,4},{3,5},{4,2},{5,3},{6,0},{7,1},{8,14},{9,15},{10,... | collective-permute-start | bytes 196616 | tf_op jit(solution)/shard_map/ppermute | solution.py:133
  14.9 5.4 %collective-permute-start.10 = (bf16[16,2048]{1,0:T(8,128)(2,1)S(1)}, bf16[16,2048]{1,0:T(8,128)(2,1)S(1)}, u32[]{:S(2)}, u32[]{:S(2)}) collective-permute-start(bf16[16,2048]{1,0:T(8,128)(2,1)S(1)} %collective-permute-done.8.refs_1_), channel_id=1, source_target_pairs={{0,6},{1,7},{2,4},{3,5},{4,2},{5,3},{6,0},{7,1},{8,14},{9,15},{10,... | collective-permute-start | bytes 196616 | tf_op jit(solution)/shard_map/ppermute | solution.py:133
  17.6 9.1 %collective-permute-start.5 = (bf16[3,16,2048]{2,1,0:T(8,128)(2,1)}, bf16[3,16,2048]{2,1,0:T(8,128)(2,1)S(1)}, u32[]{:S(2)}, u32[]{:S(2)}) collective-permute-start(bf16[3,16,2048]{2,1,0:T(8,128)(2,1)} %pad_maximum_fusion.1), channel_id=1, source_target_pairs={{0,2},{1,3},{2,0},{3,1},{4,6},{5,7},{6,4},{7,5},{8,10},{9,11},{10,... | collective-permute-start | bytes 589832 | tf_op jit(solution)/shard_map/ppermute | solution.py:133
  20.3 5.3 %collective-permute-start.11 = (bf16[4,16,2048]{2,1,0:T(8,128)(2,1)S(1)}, bf16[4,16,2048]{2,1,0:T(8,128)(2,1)S(1)}, u32[]{:S(2)}, u32[]{:S(2)}) collective-permute-start(bf16[4,16,2048]{2,1,0:T(8,128)(2,1)S(1)} %pad_maximum_fusion), channel_id=1, source_target_pairs={{0,2},{1,3},{2,0},{3,1},{4,6},{5,7},{6,4},{7,5},{8,10},{9,11},{10,... | collective-permute-start | bytes 786440 | tf_op jit(solution)/shard_map/ppermute | solution.py:133
  20.5 3.8 %collective-permute-start.4 = (bf16[16,2048]{1,0:T(8,128)(2,1)S(1)}, bf16[16,2048]{1,0:T(8,128)(2,1)S(1)}, u32[]{:S(2)}, u32[]{:S(2)}) collective-permute-start(bf16[16,2048]{1,0:T(8,128)(2,1)S(1)} %collective-permute-done.2.refs_1_), channel_id=1, source_target_pairs={{0,6},{1,7},{2,4},{3,5},{4,2},{5,3},{6,0},{7,1},{8,14},{9,15},{10,... | collective-permute-start | bytes 196616 | tf_op jit(solution)/shard_map/ppermute | solution.py:133
  24.3 2.4 %collective-permute-start.6 = (bf16[16,2048]{1,0:T(8,128)(2,1)S(1)}, bf16[16,2048]{1,0:T(8,128)(2,1)S(1)}, u32[]{:S(2)}, u32[]{:S(2)}) collective-permute-start(bf16[16,2048]{1,0:T(8,128)(2,1)S(1)} %collective-permute-done.4.refs_3_), channel_id=1, source_target_pairs={{0,2},{1,3},{2,0},{3,1},{4,6},{5,7},{6,4},{7,5},{8,10},{9,11},{10,... | collective-permute-start | bytes 196616 | tf_op jit(solution)/shard_map/ppermute | solution.py:133
